TPU v7x, 8 devices: a whole 2x2x1 slice. The times are simulated.
8 devices in a mesh: dp: 1 (over z), tp: 2 (over y), ep: 4 (over x, core).
Axes of the slice: x: 2, y: 2, z: 1, core: 2. Of those that a mesh axis runs over, the one named last changes fastest.
Arguments:
- x: bfloat16 [128, 512, 768], P(('dp', 'ep'))
- src_len: int32 [128], P(('dp', 'ep'))
- expert_idx: int32 [128, 512, 2], P(('dp', 'ep'))
- ln_gain: float32 [4, 768], replicated
- ln_bias: float32 [4, 768], replicated
- w_query: bfloat16 [2, 768, 12, 64], P(None, None, 'tp')
- b_query: float32 [2, 12, 64], P(None, 'tp')
- w_key: bfloat16 [2, 768, 12, 64], P(None, None, 'tp')
- w_value: bfloat16 [2, 768, 12, 64], P(None, None, 'tp')
- b_value: float32 [2, 12, 64], P(None, 'tp')
- w_attn_out: bfloat16 [2, 12, 64, 768], P(None, 'tp')
- b_attn_out: float32 [2, 768], replicated
- w_fc1: bfloat16 [768, 3072], P(None, 'tp')
- b_fc1: float32 [3072], P('tp')
- w_fc2: bfloat16 [3072, 768], P('tp')
- b_fc2: float32 [768], replicated
- w_router: float32 [768, 16], replicated
- w_exp_in: bfloat16 [16, 768, 3072], P('ep', None, 'tp')
- b_exp_in: float32 [16, 3072], P('ep', 'tp')
- w_exp_out: bfloat16 [16, 3072, 768], P('ep', 'tp')
- b_exp_out: float32 [16, 768], P('ep')
Outputs:
- output: bfloat16 [128, 512, 768], P(('dp', 'ep'))
All inputs are finite; a program needn't handle non-finite values.
Results may differ from a plain program's by a relative error of at most 0.0135335.
Values are sent between devices in bfloat16 or wider.
A program may use at most 1 GiB of HBM per device.

v0:
```python
import jax
import jax.numpy as jnp
from jax import lax
from jax.sharding import PartitionSpec as P

LN_EPS = 1e-5


def layer_norm(hidden, gain, shift):
    hidden = hidden.astype(jnp.float32)
    centered = hidden - jnp.mean(hidden, axis=-1, keepdims=True)
    variance = jnp.mean(centered * centered, axis=-1, keepdims=True)
    return centered * lax.rsqrt(variance + LN_EPS) * gain + shift


def attention_layer(residual, key_ok, gain, shift, w_q, b_q, w_k, w_v, b_v, w_o, b_o):
    normed = layer_norm(residual, gain, shift).astype(jnp.bfloat16)
    query = (jnp.einsum('rsd,dhk->rshk', normed, w_q, preferred_element_type=jnp.float32) + b_q).astype(jnp.bfloat16)
    keys = jnp.einsum('rsd,dhk->rshk', normed, w_k, preferred_element_type=jnp.float32).astype(jnp.bfloat16)
    values = (jnp.einsum('rsd,dhk->rshk', normed, w_v, preferred_element_type=jnp.float32) + b_v).astype(jnp.bfloat16)
    scores = jnp.einsum('rqhk,rshk->rhqs', query, keys, preferred_element_type=jnp.float32) * (w_q.shape[-1] ** -0.5)
    scores = jnp.where(key_ok[:, None, None, :], scores, -1e30)
    attn_probs = jax.nn.softmax(scores, axis=-1).astype(jnp.bfloat16)
    context = jnp.einsum('rhqs,rshk->rqhk', attn_probs, values, preferred_element_type=jnp.float32).astype(jnp.bfloat16)
    partial = jnp.einsum('rqhk,hkd->rqd', context, w_o, preferred_element_type=jnp.float32).astype(jnp.bfloat16)
    total = lax.psum(partial, 'tp')
    return (residual.astype(jnp.float32) + total.astype(jnp.float32) + b_o).astype(jnp.bfloat16)


def dense_ffn(residual, gain, shift, w_in, b_in, w_out, b_out):
    normed = layer_norm(residual, gain, shift).astype(jnp.bfloat16)
    inner = jax.nn.relu(jnp.einsum('rsd,df->rsf', normed, w_in, preferred_element_type=jnp.float32) + b_in).astype(jnp.bfloat16)
    partial = jnp.einsum('rsf,fd->rsd', inner, w_out, preferred_element_type=jnp.float32).astype(jnp.bfloat16)
    total = lax.psum(partial, 'tp')
    return (residual.astype(jnp.float32) + total.astype(jnp.float32) + b_out).astype(jnp.bfloat16)


def route_tokens(normed_f32, key_ok, expert_idx, w_router, capacity):
    tokens = key_ok.size
    num_experts = w_router.shape[1]
    logits = jnp.dot(normed_f32.reshape(tokens, -1), w_router, preferred_element_type=jnp.float32)
    valid = key_ok.reshape(tokens)
    first = expert_idx[..., 0].reshape(tokens)
    second = expert_idx[..., 1].reshape(tokens)
    logit_first = jnp.take_along_axis(logits, first[:, None], axis=1)[:, 0]
    logit_second = jnp.take_along_axis(logits, second[:, None], axis=1)[:, 0]
    gate_first = jax.nn.sigmoid(logit_first - logit_second)
    gate_second = jax.nn.sigmoid(logit_second - logit_first)
    expert_ids = jnp.arange(num_experts, dtype=jnp.int32)
    hot_first = ((first[:, None] == expert_ids) & valid[:, None]).astype(jnp.int32)
    hot_second = ((second[:, None] == expert_ids) & valid[:, None]).astype(jnp.int32)
    rank_first = jnp.cumsum(hot_first, axis=0) - 1
    rank_second = jnp.cumsum(hot_second, axis=0) - 1 + jnp.sum(hot_first, axis=0)
    slot_first = jnp.sum(rank_first * hot_first, axis=1)
    slot_second = jnp.sum(rank_second * hot_second, axis=1)
    dump_slot = num_experts * capacity
    dest_first = jnp.where(valid & (slot_first < capacity), first * capacity + slot_first, dump_slot)
    dest_second = jnp.where(valid & (slot_second < capacity), second * capacity + slot_second, dump_slot)
    return gate_first, gate_second, dest_first, dest_second


def slot_table(dest_first, dest_second, dump_slot):
    tokens = dest_first.shape[0]
    token_ids = jnp.arange(tokens, dtype=jnp.int32)
    table = jnp.full((dump_slot + 1,), tokens, jnp.int32)
    table = table.at[dest_first].set(token_ids).at[dest_second].set(token_ids)
    return table[:dump_slot]


def solution(mesh):
    ep_size = mesh.shape['ep']

    def local_fn(x, src_len, expert_idx, ln_gain, ln_bias, w_query, b_query, w_key, w_value, b_value, w_attn_out, b_attn_out, w_fc1, b_fc1, w_fc2, b_fc2, w_router, w_exp_in, b_exp_in, w_exp_out, b_exp_out):
        rows, seq_len, d_model = x.shape
        tokens = rows * seq_len
        num_experts = w_router.shape[1]
        capacity = 2 * (-(-tokens // num_experts))
        dump_slot = num_experts * capacity
        local_experts = w_exp_in.shape[0]
        key_ok = jnp.arange(seq_len)[None, :] < src_len[:, None]
        hidden = attention_layer(x, key_ok, ln_gain[0], ln_bias[0], w_query[0], b_query[0], w_key[0], w_value[0], b_value[0], w_attn_out[0], b_attn_out[0])
        hidden = dense_ffn(hidden, ln_gain[1], ln_bias[1], w_fc1, b_fc1, w_fc2, b_fc2)
        hidden = attention_layer(hidden, key_ok, ln_gain[2], ln_bias[2], w_query[1], b_query[1], w_key[1], w_value[1], b_value[1], w_attn_out[1], b_attn_out[1])
        normed_f32 = layer_norm(hidden, ln_gain[3], ln_bias[3])
        gate_first, gate_second, dest_first, dest_second = route_tokens(normed_f32, key_ok, expert_idx, w_router, capacity)
        table = slot_table(dest_first, dest_second, dump_slot)
        padded = jnp.concatenate([normed_f32.astype(jnp.bfloat16).reshape(tokens, d_model), jnp.zeros((1, d_model), jnp.bfloat16)], axis=0)
        dispatch = padded[table].reshape(num_experts, capacity, d_model)
        received = lax.all_to_all(dispatch, 'ep', 0, 0, tiled=True).reshape(ep_size, local_experts, capacity, d_model)
        inner = jax.nn.relu(jnp.einsum('gecd,edf->gecf', received, w_exp_in, preferred_element_type=jnp.float32) + b_exp_in[None, :, None, :]).astype(jnp.bfloat16)
        partial = jnp.einsum('gecf,efd->gecd', inner, w_exp_out, preferred_element_type=jnp.float32).astype(jnp.bfloat16)
        summed = lax.psum(partial, 'tp')
        expert_out = (summed.astype(jnp.float32) + b_exp_out[None, :, None, :]).astype(jnp.bfloat16)
        returned = lax.all_to_all(expert_out.reshape(num_experts, capacity, d_model), 'ep', 0, 0, tiled=True)
        flat = jnp.concatenate([returned.reshape(dump_slot, d_model), jnp.zeros((1, d_model), jnp.bfloat16)], axis=0)
        combined = gate_first[:, None] * flat[dest_first].astype(jnp.float32) + gate_second[:, None] * flat[dest_second].astype(jnp.float32)
        result = hidden.reshape(tokens, d_model).astype(jnp.float32) + combined
        return result.astype(jnp.bfloat16).reshape(rows, seq_len, d_model)

    in_specs = (P(('dp', 'ep'), None, None), P(('dp', 'ep')), P(('dp', 'ep'), None, None), P(), P(), P(None, None, 'tp', None), P(None, 'tp', None), P(None, None, 'tp', None), P(None, None, 'tp', None), P(None, 'tp', None), P(None, 'tp', None, None), P(), P(None, 'tp'), P('tp'), P('tp', None), P(), P(), P('ep', None, 'tp'), P('ep', 'tp'), P('ep', 'tp', None), P('ep', None))
    return jax.shard_map(local_fn, mesh=mesh, in_specs=in_specs, out_specs=P(('dp', 'ep'), None, None), check_vma=False)
```

profile of v0, /device:TPU:7, one launch (start us, length us, event | category | flops | bytes accessed | tf_op | source)
XLA Modules:
  0.0 6140.6 jit_solution(18093211841018376115)
XLA Ops:
  6.6 1.5 fusion.133
  8.1 1.4 fusion.153
  9.4 10.9 convert_reduce_fusion.3
  20.3 18.3 fusion.33
  38.6 0.7 slice_reduce_fusion
  39.3 17.6 convolution_convert_fusion.2
  56.9 21.7 fusion.107
  78.5 0.6 fusion.152
  79.1 18.2 add_convert_fusion.3
  97.3 83.5 %fusion.154 = (f32[32,6,512]{2,1,0:T(8,128)S(1)}, f32[32,6,512,512]{2,3,1,0:T(8,128)}) fusion(pred[32,512]{1,0:T(8,128)(4,1)S(1)} %get-tuple-element.40, bf16[32,512,6,64]{1,3,2,0:T(8,128)(2,1)} %add_convert_fusion.3, bf16[32,512,6,64]{1,3,2,0:T(8,128)(2,1)} %convolution_convert_fusion.2), kind=kOutput, calls=%fused_computation.218 | convolution fusion | flops 6643778048 | bytes 226902016 | tf_op jit(solution)/shard_map/sub | solution.py:23
  180.8 73.0 %fusion.193 = bf16[32,512,6,64]{1,3,2,0:T(8,128)(2,1)} fusion(f32[32,6,512,512]{2,3,1,0:T(8,128)} %get-tuple-element.42, f32[32,6,512]{2,1,0:T(8,128)S(1)} %get-tuple-element.41, f32[32,512,6,64]{1,3,2,0:T(8,128)} %fusion.107, f32[6,64]{1,0:T(8,128)S(1)} %bitcast.248), kind=kOutput, calls=%fused_computation.93.clone.2 | convolution fusion | flops 6561988608 | bytes 239470080 | tf_op jit(solution)/shard_map/rhqs,rshk->rqhk/dot_general | solution.py:24
  253.8 21.9 bitcast_convert_fusion.1
  275.8 0.6 slice_reduce_fusion.2
  276.4 552.6 %all-reduce.7.cloned.1.call-done = bf16[32,512,768]{2,1,0:T(8,128)(2,1)} async-done(((bf16[32,512,768]{2,1,0:T(8,128)(2,1)}), bf16[32,512,768]{2,1,0:T(8,128)(2,1)}) %all-reduce.7.cloned.1.call-update) | async-done | bytes 25165840 | tf_op jit(solution)/shard_map/psum | solution.py:26
  829.0 26.4 convert_reduce_fusion.2
  855.4 18.3 fusion.29
  873.7 54.2 maximum_convert_fusion.1.clone.4
  927.9 48.3 convolution_convert_fusion
  976.3 0.6 copy.91
  976.9 552.9 %all-reduce.9.cloned.1.call-done = bf16[32,512,768]{2,1,0:T(8,128)(2,1)} async-done(((bf16[32,512,768]{2,1,0:T(8,128)(2,1)}), bf16[32,512,768]{2,1,0:T(8,128)(2,1)}) %all-reduce.9.cloned.1.call-update) | async-done | bytes 25165840 | tf_op jit(solution)/shard_map/psum | solution.py:34
  1529.8 26.2 convert_reduce_fusion.1
  1555.9 18.3 fusion.25
  1574.3 17.9 convolution_convert_fusion.1
  1592.2 22.4 fusion.102
  1614.7 18.5 add_convert_fusion.1
  1633.2 83.8 %fusion.155 = (f32[32,6,512]{2,1,0:T(8,128)S(1)}, f32[32,6,512,512]{2,3,1,0:T(8,128)}) fusion(pred[32,512]{1,0:T(8,128)(4,1)S(1)} %copy-done.29, bf16[32,512,6,64]{1,3,2,0:T(8,128)(2,1)} %add_convert_fusion.1, bf16[32,512,6,64]{1,3,2,0:T(8,128)(2,1)} %convolution_convert_fusion.1), kind=kOutput, calls=%fused_computation.219 | convolution fusion | flops 6643778048 | bytes 226902016 | tf_op jit(solution)/shard_map/sub | solution.py:23
  1716.9 73.1 %fusion.191 = bf16[32,512,6,64]{1,3,2,0:T(8,128)(2,1)} fusion(f32[32,6,512,512]{2,3,1,0:T(8,128)} %get-tuple-element.44, f32[32,6,512]{2,1,0:T(8,128)S(1)} %get-tuple-element.43, f32[32,512,6,64]{1,3,2,0:T(8,128)} %fusion.102, f32[6,64]{1,0:T(8,128)S(1)} %bitcast.245), kind=kOutput, calls=%fused_computation.92.clone.2 | convolution fusion | flops 6561988608 | bytes 239470080 | tf_op jit(solution)/shard_map/rhqs,rshk->rqhk/dot_general | solution.py:24
  1790.1 21.9 bitcast_convert_fusion
  1813.1 0.3 reduce-window.19
  1813.5 0.4 copy.56
  1814.3 0.3 reduce-window.15
  1814.7 0.4 copy.54
  1815.2 0.9 convert_reduce_fusion.4
  1816.1 0.9 fusion.85
  1817.0 1.1 fusion.141
  1818.1 60.4 scatter_custom_fusion
  1878.5 60.4 scatter_fusion
  1939.0 426.6 %all-reduce.11.cloned.1.call-done = bf16[32,512,768]{2,1,0:T(8,128)(2,1)} async-done(((bf16[32,512,768]{2,1,0:T(8,128)(2,1)}), bf16[32,512,768]{2,1,0:T(8,128)(2,1)}) %all-reduce.11.cloned.1.call-update) | async-done | bytes 25165840 | tf_op jit(solution)/shard_map/psum | solution.py:26
  2365.6 26.0 convert_reduce_fusion
  2391.6 18.3 fusion.22
  2409.9 17.8 fusion.98
  2427.7 20.5 concatenate.6
  2448.2 156.5 %gather_fusion = bf16[32768,768]{1,0:T(8,128)(2,1)} fusion(bf16[16385,768]{1,0:T(8,128)(2,1)} %concatenate.6, s32[32768]{0:T(1024)S(1)} %fusion.123), kind=kCustom, calls=%fused_computation.2 | custom fusion | bytes 100794368 | tf_op jit(solution)/shard_map/gather | solution.py:88
  2604.6 567.0 %all_to_all.10 = bf16[16,2048,768]{2,1,0:T(8,128)(2,1)} all-to-all(bf16[16,2048,768]{2,1,0:T(8,128)(2,1)} %bitcast.218), channel_id=1, replica_groups=mesh['dp'=1,'tp'=2,'ep'=4] {'ep'}, dimensions={0} | all-to-all | bytes 100663296 | tf_op jit(solution)/shard_map/all_to_all | solution.py:89
  3171.6 89.1 %fusion.197 = bf16[4,4,2048,1536]{3,2,0,1:T(8,128)(2,1)} fusion(f32[4,1536]{1,0:T(4,128)S(1)} %copy-done.51, bf16[4,768,1536]{2,1,0:T(8,128)(2,1)} %param.40, bf16[4,4,2048,768]{3,2,1,0:T(8,128)(2,1)} %bitcast.223), kind=kOutput, calls=%fused_computation.19.clone.clone.clone.1 | convolution fusion | flops 77460406272 | bytes 160456704 | tf_op jit(solution)/shard_map/gecd,edf->gecf/dot_general | solution.py:90
  3260.7 90.4 %convert_bitcast_fusion = bf16[4,4,2048,768]{3,2,0,1:T(8,128)(2,1)} fusion(bf16[4,1536,768]{2,1,0:T(8,128)(2,1)} %param.42, bf16[4,4,2048,1536]{3,2,0,1:T(8,128)(2,1)} %fusion.197), kind=kOutput, calls=%fused_computation.78 | convolution fusion | flops 77334577152 | bytes 160432128 | tf_op jit(solution)/shard_map/gecf,efd->gecd/dot_general | solution.py:91
  3351.2 1094.5 %all-reduce.13.cloned.1.call-done = bf16[4,4,2048,768]{3,2,0,1:T(8,128)(2,1)} async-done(((bf16[4,4,2048,768]{3,2,0,1:T(8,128)(2,1)}), bf16[4,4,2048,768]{3,2,0,1:T(8,128)(2,1)}) %all-reduce.13.cloned.1.call-update) | async-done | bytes 50331664 | tf_op jit(solution)/shard_map/psum | solution.py:92
  4445.6 33.6 add_convert_fusion
  4479.2 33.8 copy.58
  4513.1 13.0 all-to-all-start.1
  4526.1 0.6 broadcast_clamp_fusion.1
  4527.0 0.4 fusion.127
  4527.5 17.8 fusion.24
  4545.3 11.5 fusion.156
  4556.8 130.6 %gather_fusion.3 = f32[16384]{0:T(1024)S(1)} fusion(f32[16384,16]{0,1:T(8,128)S(1)} %fusion.156, s32[16384]{0:T(1024)S(1)} %bitcast.216), kind=kCustom, calls=%fused_computation.clone | custom fusion | bytes 262144 | tf_op jit(solution)/shard_map/jit(take_along_axis)/gather | solution.py:45
  4687.4 130.6 %gather_fusion.4 = f32[16384]{0:T(1024)S(1)} fusion(f32[16384,16]{0,1:T(8,128)S(1)} %fusion.156, s32[16384]{0:T(1024)S(1)} %bitcast.215), kind=kCustom, calls=%fused_computation.1.clone | custom fusion | bytes 262144 | tf_op jit(solution)/shard_map/jit(take_along_axis)/gather | solution.py:46
  4818.0 0.7 divide_reduce_fusion.1
  4818.7 0.6 mul.171
  4819.3 0.6 mul.164
  4820.0 246.6 %all-to-all-done.1 = bf16[16,2048,768]{2,1,0:T(8,128)(2,1)} async-done(((bf16[16,2048,768]{2,1,0:T(8,128)(2,1)}), bf16[16,2048,768]{2,1,0:T(8,128)(2,1)}, u32[]{:S(2)}, u32[]{:S(2)}) %all-to-all-start.1) | async-done | bytes 50331680 | tf_op jit(solution)/shard_map/all_to_all | solution.py:94
  5066.6 33.5 concatenate.7
  5100.1 489.7 %gather_fusion.2 = bf16[16384,768]{1,0:T(8,128)(2,1)} fusion(bf16[32769,768]{1,0:T(8,128)(2,1)} %concatenate.7, s32[16384]{0:T(1024)S(1)} %broadcast_clamp_fusion), kind=kCustom, calls=%fused_computation.4 | custom fusion | bytes 50397184 | tf_op jit(solution)/shard_map/gather | solution.py:96
  5589.8 510.8 %gather_fusion.1 = bf16[16384,768]{1,0:T(8,128)(2,1)} fusion(bf16[32769,768]{1,0:T(8,128)(2,1)} %concatenate.7, s32[16384]{0:T(1024)S(1)} %copy-done.18), kind=kCustom, calls=%fused_computation.3 | custom fusion | bytes 50397184 | tf_op jit(solution)/shard_map/gather | solution.py:96
  6100.7 33.0 fusion.43
  (150 shorter events, 2.4 us)
Async XLA Ops:
  6.5 867.2 %copy-start = (bf16[768,1536]{1,0:T(8,128)(2,1)S(1)}, bf16[768,1536]{1,0:T(8,128)(2,1)}, u32[]{:S(2)}) copy-start(bf16[768,1536]{1,0:T(8,128)(2,1)} %param.35) | copy-start | bytes 7077892
  6.5 32.1 copy-start.31
  6.5 32.1 copy-start.32
  6.5 822.5 %all-reduce.7.cloned.1.call-start = ((), (), s32[]{:S(2)}) async-start(), calls=%async_computation.2 | async-start | bytes 50331648 | tf_op jit(solution)/shard_map/psum | solution.py:26
  6.5 32.7 copy-start.44
  8.1 89.2 %copy-start.28 = (pred[32,512]{1,0:T(8,128)(4,1)}, pred[32,512]{1,0:T(8,128)(4,1)S(1)}, u32[]{:S(2)}) copy-start(pred[32,512]{1,0:T(8,128)(4,1)S(1)} %get-tuple-element.40) | copy-start | bytes 49156
  39.3 17.6 copy-start.46
  56.9 21.7 copy-start.36
  56.9 22.3 copy-start.48
  253.8 21.9 copy-start.35
  275.7 1254.0 %all-reduce.9.cloned.1.call-start = ((), (), s32[]{:S(2)}) async-start(), calls=%async_computation.3 | async-start | bytes 50331648 | tf_op jit(solution)/shard_map/psum | solution.py:34
  829.0 44.7 copy-start.40
  829.0 44.7 copy-start.41
  829.0 44.7 copy-start.52
  927.9 48.3 copy-start.33
  927.9 48.4 copy-start.34
  927.9 601.8 %copy-start.37 = (f32[768]{0:T(1024)S(1)}, f32[768]{0:T(1024)}, u32[]{:S(2)}) copy-start(f32[768]{0:T(1024)} %param.38) | copy-start | bytes 9220
  976.2 1389.4 %all-reduce.11.cloned.1.call-start = ((), (), s32[]{:S(2)}) async-start(), calls=%async_computation.4 | async-start | bytes 50331648 | tf_op jit(solution)/shard_map/psum | solution.py:26
  976.9 597.4 %copy-start.38 = (f32[768]{0:T(1024)S(1)}, f32[768]{0:T(1024)}, u32[]{:S(2)}) copy-start(f32[768]{0:T(1024)} %get-tuple-element.17) | copy-start | bytes 9220
  976.9 597.4 %copy-start.39 = (f32[768]{0:T(1024)S(1)}, f32[768]{0:T(1024)}, u32[]{:S(2)}) copy-start(f32[768]{0:T(1024)} %get-tuple-element.45) | copy-start | bytes 9220
  976.9 597.4 %copy-start.45 = (bf16[2,768,6,64]{1,3,2,0:T(8,128)(2,1)S(1)}, bf16[2,768,6,64]{1,3,2,0:T(8,128)(2,1)}, u32[]{:S(2)}) copy-start(bf16[2,768,6,64]{1,3,2,0:T(8,128)(2,1)} %param.30) | copy-start | bytes 3538948
  1574.3 18.0 copy-start.47
  1592.2 22.4 copy-start.49
  1614.7 18.5 copy-start.29
  1633.2 83.8 %copy-start.42 = (f32[1,6,64]{2,1,0:T(8,128)S(1)}, f32[1,6,64]{2,1,0:T(8,128)}, u32[]{:S(2)}) copy-start(f32[1,6,64]{2,1,0:T(8,128)} %copy.91) | copy-start | bytes 4612
  1716.9 73.1 %copy-start.50 = (bf16[2,6,64,768]{3,2,1,0:T(8,128)(2,1)S(1)}, bf16[2,6,64,768]{3,2,1,0:T(8,128)(2,1)}, u32[]{:S(2)}) copy-start(bf16[2,6,64,768]{3,2,1,0:T(8,128)(2,1)} %param.33) | copy-start | bytes 3538948
  1790.1 22.2 copy-start.19
  1790.1 22.4 copy-start.43
  1790.1 23.9 copy-start.21
  1790.1 25.1 copy-start.20
  1812.0 2633.6 %all-reduce.13.cloned.1.call-start = ((), (), s32[]{:S(2)}) async-start(), calls=%async_computation.5 | async-start | bytes 100663296 | tf_op jit(solution)/shard_map/psum | solution.py:92
  1812.3 126.6 %copy-start.2 = (s32[32,512,1]{1,2,0:T(1,128)}, s32[32,512,1]{1,2,0:T(1,128)S(1)}, u32[]{:S(2)}) copy-start(s32[32,512,1]{1,2,0:T(1,128)S(1)} %get-tuple-element.26) | copy-start | bytes 196612
  1812.4 126.6 %copy-start.4 = (s32[32,512,1]{1,2,0:T(1,128)}, s32[32,512,1]{1,2,0:T(1,128)S(1)}, u32[]{:S(2)}) copy-start(s32[32,512,1]{1,2,0:T(1,128)S(1)} %get-tuple-element.27) | copy-start | bytes 196612
  1818.1 60.4 copy-start.16
  1818.1 120.8 %copy-start.8 = (s32[16384,1]{0,1:T(1,128)}, s32[16384,1]{0,1:T(1,128)S(1)}, u32[]{:S(2)}) copy-start(s32[16384,1]{0,1:T(1,128)S(1)} %get-tuple-element.31) | copy-start | bytes 196612
  1878.5 487.0 %copy-start.27 = (f32[768]{0:T(1024)S(1)}, f32[768]{0:T(1024)}, u32[]{:S(2)}) copy-start(f32[768]{0:T(1024)} %get-tuple-element.18) | copy-start | bytes 9220
  2365.6 44.3 copy-start.23
  2365.6 44.3 copy-start.25
  2391.5 56.6 copy-start.6
  2409.9 38.3 copy-start.10
  2604.6 567.0 %copy-start.51 = (f32[4,1536]{1,0:T(4,128)S(1)}, f32[4,1536]{1,0:T(4,128)}, u32[]{:S(2)}) copy-start(f32[4,1536]{1,0:T(4,128)} %param.41) | copy-start | bytes 73732
  3351.2 1094.5 %copy-start.30 = (f32[4,768]{1,0:T(4,128)S(1)}, f32[4,768]{1,0:T(4,128)}, u32[]{:S(2)}) copy-start(f32[4,768]{1,0:T(4,128)} %param.43) | copy-start | bytes 36868
  4513.0 13.1 copy-start.9
  4513.0 13.1 copy-start.17
  4513.0 13.8 copy-start.14
  4513.0 13.8 copy-start.15
  4513.0 14.4 copy-start.7
  4513.0 14.4 copy-start.11
  4513.0 14.4 copy-start.24
  4513.1 14.4 copy-start.26
  4513.1 553.5 %all-to-all-start.1 = ((bf16[16,2048,768]{2,1,0:T(8,128)(2,1)}), bf16[16,2048,768]{2,1,0:T(8,128)(2,1)}, u32[]{:S(2)}, u32[]{:S(2)}) async-start(bf16[16,2048,768]{2,1,0:T(8,128)(2,1)} %bitcast.217), calls=%async_computation.1 | async-start | bytes 100663296 | tf_op jit(solution)/shard_map/all_to_all | solution.py:94
  4526.1 19.2 copy-start.22
  4687.4 130.6 %copy-start.3 = (s32[32,512,1]{1,2,0:T(1,128)S(1)}, s32[32,512,1]{1,2,0:T(1,128)}, u32[]{:S(2)}) copy-start(s32[32,512,1]{1,2,0:T(1,128)} %copy-done.2) | copy-start | bytes 196612
  4687.4 130.6 %copy-start.5 = (s32[32,512,1]{1,2,0:T(1,128)S(1)}, s32[32,512,1]{1,2,0:T(1,128)}, u32[]{:S(2)}) copy-start(s32[32,512,1]{1,2,0:T(1,128)} %copy-done.4) | copy-start | bytes 196612
  5100.1 489.7 %copy-start.18 = (s32[16384]{0:T(1024)S(1)}, s32[16384]{0:T(1024)}, u32[]{:S(2)}) copy-start(s32[16384]{0:T(1024)} %broadcast_clamp_fusion.1) | copy-start | bytes 196612
  5589.8 510.9 %copy-start.12 = (f32[32,512]{1,0:T(8,128)S(1)}, f32[32,512]{1,0:T(8,128)}, u32[]{:S(2)}) copy-start(f32[32,512]{1,0:T(8,128)} %mul.171) | copy-start | bytes 196612
  5589.8 510.9 %copy-start.13 = (f32[32,512]{1,0:T(8,128)S(1)}, f32[32,512]{1,0:T(8,128)}, u32[]{:S(2)}) copy-start(f32[32,512]{1,0:T(8,128)} %mul.164) | copy-start | bytes 196612
  6100.7 33.0 copy-start.1
Sparse Core Ops, SparseCore 0:
  275.8 553.1 all-reduce.6
  976.3 553.3 all-reduce.8
  1812.1 553.3 all-reduce.10
  3351.3 1094.2 all-reduce.12
where the time goes:
time: 6190 us; the launch traced here: 6140 us
  waiting for transfers between devices  2870 us (46%)
  local copies, waits for them, and re-layouts  1630 us (26%)
  matrix products  767 us (12%)
  blocking collectives  567 us (9%)
  other arithmetic  272 us (4%)
    psum x1, waiting for transfers between devices, local_fn(): summed = lax.psum(partial, 'tp')  1090 us
    psum x2, waiting for transfers between devices, attention_layer(): total = lax.psum(partial, 'tp')  979 us
    all_to_all x1, blocking collectives, local_fn(): lax.all_to_all(dispatch, 'ep', 0, 0, tiled=True)  567 us
    psum x1, waiting for transfers between devices, dense_ffn(): total = lax.psum(partial, 'tp')  553 us
    gather x1, local copies, waits for them, and re-layouts, local_fn(): flat[dest_first].astype(jnp.float32)  511 us
    gather x1, local copies, waits for them, and re-layouts, local_fn(): flat[dest_second].astype(jnp.float32)  490 us
    all_to_all x1, waiting for transfers between devices, local_fn(): lax.all_to_all(expert_out.reshape(num_experts, capacity, d_model), 'ep',...  247 us
    sub x2, matrix products, attention_layer(): attn_probs = jax.nn.softmax(scores, axis=-1).astype(jnp.bfloat16)  167 us
  transfers between devices with their start and end apart: 5, of which 5 were waited for; matrix products, arithmetic and copies ran while one was open for 7% of the time, Pallas kernels for 0%

commit v1 on v0

v1 whole, which is shorter than its diff:
```python
import functools

import jax
import jax.numpy as jnp
from jax import lax
from jax.experimental import pallas as pl
from jax.experimental.pallas import tpu as pltpu
from jax.sharding import PartitionSpec as P

LN_EPS = 1e-5
TILE_ROWS = 256
CHUNKS = 4
SECTION_SIZES = (3072, 3584)


def layer_norm(hidden, gain, shift):
    hidden = hidden.astype(jnp.float32)
    centered = hidden - jnp.mean(hidden, axis=-1, keepdims=True)
    variance = jnp.mean(centered * centered, axis=-1, keepdims=True)
    return centered * lax.rsqrt(variance + LN_EPS) * gain + shift


def attention_layer(residual, key_ok, gain, shift, w_q, b_q, w_k, w_v, b_v, w_o, b_o):
    normed = layer_norm(residual, gain, shift).astype(jnp.bfloat16)
    query = (jnp.einsum('rsd,tdhk->rsthk', normed, w_q, preferred_element_type=jnp.float32) + b_q).astype(jnp.bfloat16)
    keys = jnp.einsum('rsd,tdhk->rsthk', normed, w_k, preferred_element_type=jnp.float32).astype(jnp.bfloat16)
    values = (jnp.einsum('rsd,tdhk->rsthk', normed, w_v, preferred_element_type=jnp.float32) + b_v).astype(jnp.bfloat16)
    scores = jnp.einsum('rqthk,rsthk->rthqs', query, keys, preferred_element_type=jnp.float32) * (w_q.shape[-1] ** -0.5)
    scores = jnp.where(key_ok[:, None, None, None, :], scores, -1e30)
    attn_probs = jax.nn.softmax(scores, axis=-1).astype(jnp.bfloat16)
    context = jnp.einsum('rthqs,rsthk->rqthk', attn_probs, values, preferred_element_type=jnp.float32).astype(jnp.bfloat16)
    total = jnp.einsum('rqthk,thkd->rqd', context, w_o, preferred_element_type=jnp.float32)
    return (residual.astype(jnp.float32) + total + b_o).astype(jnp.bfloat16)


def dense_ffn(residual, gain, shift, w_in, b_in, w_out, b_out):
    normed = layer_norm(residual, gain, shift).astype(jnp.bfloat16)
    inner = jax.nn.relu(jnp.einsum('rsd,tdf->rstf', normed, w_in, preferred_element_type=jnp.float32) + b_in).astype(jnp.bfloat16)
    total = jnp.einsum('rstf,tfd->rsd', inner, w_out, preferred_element_type=jnp.float32)
    return (residual.astype(jnp.float32) + total + b_out).astype(jnp.bfloat16)


def expert_kernel(visit_tile, visit_expert, visit_lo, visit_hi, n_visits, x_ref, w_in, b_in, w_out, b_out, o_ref):
    step = pl.program_id(0)

    @pl.when(step < n_visits[0])
    def _():
        rows = x_ref[...]
        total = b_out[0]
        for part in range(w_in.shape[0]):
            inner = jnp.dot(rows, w_in[part, 0], preferred_element_type=jnp.float32) + b_in[part, 0]
            inner = jnp.maximum(inner, 0.0).astype(jnp.bfloat16)
            total = total + jnp.dot(inner, w_out[part, 0], preferred_element_type=jnp.float32)
        row = lax.broadcasted_iota(jnp.int32, total.shape, 0)
        inside = (row >= visit_lo[step]) & (row < visit_hi[step])
        o_ref[...] = jnp.where(inside, total, o_ref[...].astype(jnp.float32)).astype(jnp.bfloat16)


def plan_visits(counts, max_visits):
    ends = jnp.cumsum(counts)
    starts = ends - counts
    tiles = jnp.where(counts > 0, (ends - 1) // TILE_ROWS - starts // TILE_ROWS + 1, 0)
    visit_ends = jnp.cumsum(tiles)
    n_visits = visit_ends[-1:]
    step = jnp.minimum(jnp.arange(max_visits, dtype=jnp.int32), jnp.maximum(n_visits - 1, 0))
    expert = jnp.minimum(jnp.sum(step[:, None] >= visit_ends[None, :], axis=1), counts.shape[0] - 1).astype(jnp.int32)
    hot = expert[:, None] == jnp.arange(counts.shape[0], dtype=jnp.int32)

    def pick(values):
        return jnp.sum(jnp.where(hot, values, 0), axis=1)

    tile = pick(starts // TILE_ROWS - (visit_ends - tiles)) + step
    base = tile * TILE_ROWS
    return tile, expert, pick(starts) - base, pick(ends) - base, n_visits


def expert_ffn(rows, plan, w_in, b_in, w_out, b_out):
    count, d_model = rows.shape
    parts, local_experts, _, hidden = w_in.shape
    visits = count // TILE_ROWS + local_experts

    def row_map(i, tile, expert, lo, hi, n):
        return (tile[i], 0)

    def weight_map(i, tile, expert, lo, hi, n):
        return (0, expert[i], 0, 0)

    return pl.pallas_call(
        expert_kernel,
        grid_spec=pltpu.PrefetchScalarGridSpec(
            num_scalar_prefetch=5,
            grid=(visits,),
            in_specs=[
                pl.BlockSpec((TILE_ROWS, d_model), row_map),
                pl.BlockSpec((parts, 1, d_model, hidden), weight_map),
                pl.BlockSpec((parts, 1, 1, hidden), weight_map),
                pl.BlockSpec((parts, 1, hidden, d_model), weight_map),
                pl.BlockSpec((1, 1, d_model), lambda i, tile, expert, lo, hi, n: (expert[i], 0, 0)),
            ],
            out_specs=pl.BlockSpec((TILE_ROWS, d_model), row_map),
        ),
        out_shape=jax.ShapeDtypeStruct((count, d_model), jnp.bfloat16),
        compiler_params=pltpu.CompilerParams(dimension_semantics=('arbitrary',)),
        cost_estimate=pl.CostEstimate(flops=4 * count * d_model * hidden * parts, bytes_accessed=4 * count * d_model, transcendentals=0),
    )(*plan, rows, w_in, b_in[:, :, None, :], w_out, b_out[:, None, :])


def exclusive_sum(values, axis=0):
    return jnp.cumsum(values, axis=axis) - values


def solution(mesh):
    ep_size = mesh.shape['ep']
    tp_size = mesh.shape['tp']

    def local_fn(x, src_len, expert_idx, ln_gain, ln_bias, w_query, b_query, w_key, w_value, b_value, w_attn_out, b_attn_out, w_fc1, b_fc1, w_fc2, b_fc2, w_router, w_exp_in, b_exp_in, w_exp_out, b_exp_out):
        rows, seq_len, d_model = x.shape
        tokens = rows * seq_len
        num_experts = w_router.shape[1]
        capacity = 2 * (-(-tokens // num_experts))
        local_experts = w_exp_in.shape[0]
        half_rows = rows // tp_size
        half = half_rows * seq_len
        me_t = lax.axis_index('tp')
        me_e = lax.axis_index('ep')

        gather = functools.partial(lax.all_gather, axis_name='tp', axis=0, tiled=False)
        small = jnp.concatenate([v.reshape(-1) for v in (b_query, b_value, b_fc1, b_exp_in)])
        small = gather(small)
        cuts = [0]
        for v in (b_query, b_value, b_fc1, b_exp_in):
            cuts.append(cuts[-1] + v.size)
        full_b_query, full_b_value, full_b_fc1, full_b_exp_in = [
            small[:, lo:hi].reshape((tp_size,) + v.shape)
            for v, lo, hi in zip((b_query, b_value, b_fc1, b_exp_in), cuts[:-1], cuts[1:])]
        heads = w_query.shape[2]
        head_dim = w_query.shape[3]
        inner_dim = heads * head_dim

        def gather_attention(j):
            packed = jnp.stack([w[j].reshape(d_model, inner_dim) for w in (w_query, w_key, w_value)] + [w_attn_out[j].reshape(inner_dim, d_model).reshape(d_model, inner_dim)])
            whole = gather(packed)
            w_q, w_k, w_v = [whole[:, i].reshape(tp_size, d_model, heads, head_dim) for i in range(3)]
            return w_q, w_k, w_v, whole[:, 3].reshape(tp_size, inner_dim, d_model).reshape(tp_size, heads, head_dim, d_model)

        attn0 = gather_attention(0)
        full_fc1 = gather(w_fc1)
        full_fc2 = gather(w_fc2)
        attn1 = gather_attention(1)
        full_exp_in = gather(w_exp_in)
        full_exp_out = gather(w_exp_out)

        def mine(array):
            return lax.dynamic_index_in_dim(array.reshape((half_rows, tp_size) + array.shape[1:]), me_t, 1, keepdims=False)

        key_ok_all = jnp.arange(seq_len)[None, :] < src_len[:, None]
        expert_ids = jnp.arange(num_experts, dtype=jnp.int32)
        valid = key_ok_all.reshape(tokens)
        first = expert_idx[..., 0].reshape(tokens)
        second = expert_idx[..., 1].reshape(tokens)
        hot_first = ((first[:, None] == expert_ids) & valid[:, None]).astype(jnp.int32)
        hot_second = ((second[:, None] == expert_ids) & valid[:, None]).astype(jnp.int32)
        sum_first = jnp.cumsum(hot_first, axis=0)
        sum_second = jnp.cumsum(hot_second, axis=0) + sum_first[-1]
        kept_first = jnp.where(sum_first <= capacity, hot_first, 0).reshape(rows, seq_len, num_experts)
        kept_second = jnp.where(sum_second <= capacity, hot_second, 0).reshape(rows, seq_len, num_experts)
        part_first = jnp.sum(kept_first.reshape(half_rows, tp_size, seq_len, num_experts), axis=(0, 2))
        part_second = jnp.sum(kept_second.reshape(half_rows, tp_size, seq_len, num_experts), axis=(0, 2))
        all_counts = lax.all_gather(part_first + part_second, 'ep')
        most = jnp.max(jnp.sum(all_counts.reshape(ep_size, tp_size, ep_size, local_experts), axis=3))
        my_counts = lax.dynamic_index_in_dim(part_first + part_second, me_t, 0, keepdims=False).reshape(ep_size, local_experts)
        my_counts_first = lax.dynamic_index_in_dim(part_first, me_t, 0, keepdims=False)
        offsets = exclusive_sum(my_counts, axis=1).reshape(num_experts)
        my_first = mine(kept_first).reshape(half, num_experts)
        my_second = mine(kept_second).reshape(half, num_experts)
        pos_first = jnp.sum((jnp.cumsum(my_first, axis=0) - 1 + offsets) * my_first, axis=1)
        pos_second = jnp.sum((jnp.cumsum(my_second, axis=0) - 1 + offsets + my_counts_first) * my_second, axis=1)
        keep_first = jnp.sum(my_first, axis=1) > 0
        keep_second = jnp.sum(my_second, axis=1) > 0
        choice_first = mine(expert_idx[..., 0]).reshape(half)
        choice_second = mine(expert_idx[..., 1]).reshape(half)
        dest_first = (choice_first // local_experts) ^ me_e
        dest_second = (choice_second // local_experts) ^ me_e
        most_rows = half
        token_ids = jnp.arange(half, dtype=jnp.int32)
        dump = ep_size * most_rows
        table = jnp.zeros((dump,), jnp.int32).at[jnp.concatenate([
            jnp.where(keep_first, dest_first * most_rows + pos_first, dump),
            jnp.where(keep_second, dest_second * most_rows + pos_second, dump),
        ])].set(jnp.concatenate([token_ids, token_ids]), mode='drop').reshape(ep_size, most_rows)
        swap = {s: [(i, i ^ s) for i in range(ep_size)] for s in range(1, ep_size)}
        tables = [table[0]] + [lax.ppermute(table[s], 'ep', swap[s]) for s in range(1, ep_size)]
        section_counts = lax.dynamic_index_in_dim(lax.dynamic_index_in_dim(all_counts, me_t, 1, keepdims=False).reshape(ep_size, ep_size, local_experts), me_e, 1, keepdims=False)
        max_visits = most_rows // TILE_ROWS + local_experts
        plans = [plan_visits(lax.dynamic_index_in_dim(section_counts, me_e ^ s, 0, keepdims=False), max_visits) for s in range(ep_size)]

        x_half = mine(x)
        key_ok = mine(key_ok_all)
        chunk = half_rows // CHUNKS
        hidden_parts, logit_parts = [], []
        sections = [[] for _ in range(ep_size)]
        for c in range(CHUNKS):
            part = slice(c * chunk, (c + 1) * chunk)
            hidden = attention_layer(x_half[part], key_ok[part], ln_gain[0], ln_bias[0], attn0[0], full_b_query[:, 0], attn0[1], attn0[2], full_b_value[:, 0], attn0[3], b_attn_out[0])
            hidden = dense_ffn(hidden, ln_gain[1], ln_bias[1], full_fc1, full_b_fc1.reshape(tp_size, -1), full_fc2, b_fc2)
            hidden = attention_layer(hidden, key_ok[part], ln_gain[2], ln_bias[2], attn1[0], full_b_query[:, 1], attn1[1], attn1[2], full_b_value[:, 1], attn1[3], b_attn_out[1])
            normed_f32 = layer_norm(hidden, ln_gain[3], ln_bias[3]).reshape(chunk * seq_len, d_model)
            logit_parts.append(jnp.dot(normed_f32, w_router, preferred_element_type=jnp.float32))
            hidden_parts.append(hidden.reshape(chunk * seq_len, d_model))
            sent = normed_f32.astype(jnp.bfloat16)
            across = lax.ppermute(sent, 'ep', swap[2])
            sections[0].append(sent)
            sections[1].append(lax.ppermute(sent, 'ep', swap[1]))
            sections[2].append(across)
            sections[3].append(lax.ppermute(across, 'ep', swap[1]))

        logits = jnp.concatenate(logit_parts, axis=0)
        logit_first = jnp.sum(jnp.where(choice_first[:, None] == expert_ids, logits, 0.0), axis=1)
        logit_second = jnp.sum(jnp.where(choice_second[:, None] == expert_ids, logits, 0.0), axis=1)
        gate_first = jnp.where(keep_first, jax.nn.sigmoid(logit_first - logit_second), 0.0)
        gate_second = jnp.where(keep_second, jax.nn.sigmoid(logit_second - logit_first), 0.0)
        section_rows = [jnp.concatenate(parts, axis=0) for parts in sections]

        def experts(size):
            def run():
                back = [None] * ep_size
                for s in (3, 2, 1, 0):
                    rows_in = section_rows[s][tables[s][:size]]
                    out = expert_ffn(rows_in, plans[s], full_exp_in, full_b_exp_in, full_exp_out, b_exp_out)
                    back[s] = lax.ppermute(out, 'ep', swap[s]) if s else out
                flat = jnp.concatenate(back, axis=0)
                rows_first = flat[jnp.where(keep_first, dest_first * size + pos_first, 0)].astype(jnp.float32)
                rows_second = flat[jnp.where(keep_second, dest_second * size + pos_second, 0)].astype(jnp.float32)
                combined = jnp.where(keep_first[:, None], gate_first[:, None] * rows_first, 0.0) + jnp.where(keep_second[:, None], gate_second[:, None] * rows_second, 0.0)
                return (jnp.concatenate(hidden_parts, axis=0).astype(jnp.float32) + combined).astype(jnp.bfloat16)
            return run

        sizes = [size for size in SECTION_SIZES if size < most_rows] + [most_rows]
        level = sum((most > size).astype(jnp.int32) for size in sizes[:-1])
        result = lax.switch(level, [experts(size) for size in sizes])
        return lax.all_gather(result.reshape(half_rows, 1, seq_len, d_model), 'tp', axis=1, tiled=True).reshape(rows, seq_len, d_model)

    in_specs = (P(('dp', 'ep'), None, None), P(('dp', 'ep')), P(('dp', 'ep'), None, None), P(), P(), P(None, None, 'tp', None), P(None, 'tp', None), P(None, None, 'tp', None), P(None, None, 'tp', None), P(None, 'tp', None), P(None, 'tp', None, None), P(), P(None, 'tp'), P('tp'), P('tp', None), P(), P(), P('ep', None, 'tp'), P('ep', 'tp'), P('ep', 'tp', None), P('ep', None))
    return jax.shard_map(local_fn, mesh=mesh, in_specs=in_specs, out_specs=P(('dp', 'ep'), None, None), check_vma=False)
```

time: 6190 us -> 1940 us (0.31)
  waiting for transfers between devices: 2870 us -> 585 us
  local copies, waits for them, and re-layouts: 1630 us -> 314 us
  blocking collectives: 567 us -> 11.4 us
  Pallas kernels: 0 us -> 174 us
  matrix products: 767 us -> 639 us
  other arithmetic: 272 us -> 154 us
    psum x4 -> x0, waiting for transfers between devices: 2630 us -> none  [the longest x1 1090 us: local_fn(): summed = lax.psum(partial, 'tp')]
    gather x5 -> x6, local copies, waits for them, and re-layouts: 1420 us -> 176 us  [the longest x4 83.4 us: run(): rows_in = section_rows[s][tables[s][:size]]]
    all_to_all x1 -> x0, blocking collectives: 567 us -> none  [local_fn(): lax.all_to_all(dispatch, 'ep', 0, 0, tiled=True)]
    all_gather x0 -> x7, waiting for transfers between devices: none -> 331 us  [the longest x1 295 us: local_fn(): lax.all_gather(result.reshape(half_rows, 1, seq_len, d_model), 'tp', axis...]
    ppermute x0 -> x18, waiting for transfers between devices: none -> 252 us  [the longest x4 182 us: local_fn(): across = lax.ppermute(sent, 'ep', swap[2])]
    all_to_all x1 -> x0, waiting for transfers between devices: 247 us -> none  [local_fn(): lax.all_to_all(expert_out.reshape(num_experts, capacity, d_model), 'ep',...]
    pallas_call x0 -> x4, Pallas kernels: none -> 174 us  [expert_ffn(): pl.pallas_call(expert_kernel, grid_spec=pltpu.PrefetchScalarGridSpec(num_...]
    dot_general x15 -> x40, matrix products: 600 us -> 431 us  [the longest x8 179 us: attention_layer(): jnp.einsum('rqthk,thkd->rqd', context, w_o, preferred_element_type=jnp.fl...]
  transfers between devices with their start and end apart: 5 -> 25, of which waited for: 5 -> 8; matrix products, arithmetic and copies ran while one was open for 7% -> 47% of each run, Pallas kernels for 0% -> 7%
where the time goes in v1:
time: 1940 us; the launch traced here: 1930 us
  matrix products  639 us (33%)
  waiting for transfers between devices  585 us (30%)
  local copies, waits for them, and re-layouts  314 us (16%)
  Pallas kernels  174 us (9%)
  other arithmetic  154 us (8%)
  starting transfers between devices  25.1 us (1%)
  between operations  19.8 us (1%)
    all_gather x1, waiting for transfers between devices, local_fn(): lax.all_gather(result.reshape(half_rows, 1, seq_len, d_model), 'tp', axis...  295 us
    sub x8, matrix products, attention_layer(): attn_probs = jax.nn.softmax(scores, axis=-1).astype(jnp.bfloat16)  207 us
    ppermute x4, waiting for transfers between devices, local_fn(): across = lax.ppermute(sent, 'ep', swap[2])  182 us
    dot_general x8, matrix products, attention_layer(): jnp.einsum('rqthk,thkd->rqd', context, w_o, preferred_element_type=jnp.fl...  179 us
    pallas_call x4, Pallas kernels, expert_ffn(): pl.pallas_call(expert_kernel, grid_spec=pltpu.PrefetchScalarGridSpec(num_...  174 us
    dot_general x4, matrix products, dense_ffn(): jnp.einsum('rstf,tfd->rsd', inner, w_out, preferred_element_type=jnp.floa...  103 us
    gather x4, local copies, waits for them, and re-layouts, run(): rows_in = section_rows[s][tables[s][:size]]  83.4 us
    ppermute x3, waiting for transfers between devices, run(): back[s] = lax.ppermute(out, 'ep', swap[s]) if s else out  70.7 us
  transfers between devices with their start and end apart: 25, of which 8 were waited for; matrix products, arithmetic and copies ran while one was open for 47% of the time, Pallas kernels for 7%

profile of v1, /device:TPU:7, one launch (start us, length us, event | category | flops | bytes accessed | tf_op | source)
XLA Modules:
  0.0 1931.5 jit_solution(4278770292460847068)
XLA Ops:
  35.4 6.2 all-gather.8
  65.5 7.1 fusion.147
  108.1 6.9 convolution_convert_fusion.1
  115.0 6.4 add_convert_fusion.2
  121.4 6.5 add_convert_fusion.6
  127.9 6.5 convolution_convert_fusion.3
  136.0 6.8 add_convert_fusion.3
  142.9 6.5 add_convert_fusion.7
  150.6 25.6 %fusion.537 = (f32[4,2,6,512]{3,2,1,0:T(8,128)S(1)}, f32[4,2,6,512,512]{3,4,2,1,0:T(8,128)}) fusion(pred[4,512]{1,0:T(4,128)(4,1)S(1)} %copy-done.167, bf16[4,512,2,6,64]{1,4,3,2,0:T(8,128)(2,1)} %add_convert_fusion.2, bf16[4,512,2,6,64]{1,4,3,2,0:T(8,128)(2,1)} %convolution_convert_fusion.1), kind=kOutput, calls=%fused_computation.737 | convolution fusion | flops 1660944896 | bytes 56723456 | tf_op jit(solution)/shard_map/sub | solution.py:30
  176.3 22.5 %convert_reduce_fusion.1 = (f32[4,512]{1,0:T(4,128)S(1)}, bf16[4,512,768]{2,1,0:T(8,128)(2,1)S(1)}) fusion(f32[768]{0:T(1024)S(1)} %copy-done.143, bf16[4,512,2,6,64]{1,4,3,2,0:T(8,128)(2,1)} %add_convert_fusion.3, bf16[16,2,512,768]{3,2,1,0:T(8,128)(2,1)} %bitcast.731, s32[]{:T(128)S(6)} %add.1106, s32[]{:T(128)S(6)} %select_n.440, ...), kind=kOutput, calls=%fused_computation.154 | convolution fusion | flops 4062705664 | bytes 61058056 | tf_op jit(solution)/shard_map/rqthk,thkd->rqd/dot_general | solution.py:32
  201.7 25.3 %convert_reduce_fusion = (f32[4,512]{1,0:T(4,128)S(1)}, bf16[4,512,768]{2,1,0:T(8,128)(2,1)S(1)}) fusion(f32[768]{0:T(1024)S(1)} %copy-done.192, bf16[2,1536,768,1]{2,1,0,3:T(8,128)(2,1)} %bitcast.834, bf16[2,768,1536,1]{2,1,0,3:T(8,128)(2,1)} %bitcast.830, f32[2,1536]{1,0:T(2,128)S(1)} %copy-done.104, bf16[4,512,768]{2,1,0:T(8,128)(2,1)} %copy-done.19, ...), kind=kOutput, calls=%fused_computation.151 | convolution fusion | flops 19365099520 | bytes 15774720 | tf_op jit(solution)/shard_map/rstf,tfd->rsd/dot_general | solution.py:39
  229.3 34.0 %all-gather.25.cloned.1.call-done = bf16[8,768,384]{2,1,0:T(8,128)(2,1)} async-done(((bf16[4,768,384]{2,1,0:T(8,128)(2,1)}), bf16[8,768,384]{2,1,0:T(8,128)(2,1)}) %all-gather.25.cloned.1.call-update) | async-done | bytes 4718608 | tf_op jit(solution)/shard_map/all_gather | solution.py:142
  270.5 25.8 %fusion.529 = (f32[4,2,6,512]{3,2,1,0:T(8,128)S(1)}, f32[4,2,6,512,512]{3,4,2,1,0:T(8,128)}) fusion(pred[4,512]{1,0:T(4,128)(4,1)S(1)} %copy-done.165, bf16[4,512,2,6,64]{1,4,3,2,0:T(8,128)(2,1)} %add_convert_fusion.6, bf16[4,512,2,6,64]{1,4,3,2,0:T(8,128)(2,1)} %convolution_convert_fusion.3), kind=kOutput, calls=%fused_computation.735 | convolution fusion | flops 1660944896 | bytes 56723456 | tf_op jit(solution)/shard_map/sub | solution.py:30
  296.3 22.1 %convert_reduce_fusion.4 = (f32[4,512]{1,0:T(4,128)S(1)}, bf16[4,512,768]{2,1,0:T(8,128)(2,1)S(1)}) fusion(f32[768]{0:T(1024)S(1)} %copy-done.143, bf16[4,512,2,6,64]{1,4,3,2,0:T(8,128)(2,1)} %add_convert_fusion.7, bf16[16,2,512,768]{3,2,1,0:T(8,128)(2,1)} %bitcast.732, s32[]{:T(128)S(6)} %add.1105, s32[]{:T(128)S(6)} %select_n.440, ...), kind=kOutput, calls=%fused_computation.163 | convolution fusion | flops 4062705664 | bytes 61058056 | tf_op jit(solution)/shard_map/rqthk,thkd->rqd/dot_general | solution.py:32
  320.2 26.8 %convert_reduce_fusion.3 = (f32[4,512]{1,0:T(4,128)S(1)}, bf16[4,512,768]{2,1,0:T(8,128)(2,1)}) fusion(f32[768]{0:T(1024)S(1)} %copy-done.192, bf16[2,1536,768,1]{2,1,0,3:T(8,128)(2,1)} %bitcast.835, bf16[2,768,1536,1]{2,1,0,3:T(8,128)(2,1)} %bitcast.831, f32[2,1536]{1,0:T(2,128)S(1)} %copy-done.104, bf16[4,512,768]{2,1,0:T(8,128)(2,1)} %copy-done.20, ...), kind=kOutput, calls=%fused_computation.160 | convolution fusion | flops 19365099520 | bytes 15774720 | tf_op jit(solution)/shard_map/rstf,tfd->rsd/dot_general | solution.py:39
  350.1 5.8 convolution_convert_fusion
  370.3 6.8 add_convert_fusion.1
  381.7 6.5 add_convert_fusion.10
  388.3 6.5 convolution_convert_fusion.5
  394.8 6.5 add_convert_fusion.11
  401.2 25.8 %fusion.521 = (f32[4,2,6,512]{3,2,1,0:T(8,128)S(1)}, f32[4,2,6,512,512]{3,4,2,1,0:T(8,128)}) fusion(pred[4,512]{1,0:T(4,128)(4,1)S(1)} %copy-done.163, bf16[4,512,2,6,64]{1,4,3,2,0:T(8,128)(2,1)} %add_convert_fusion.10, bf16[4,512,2,6,64]{1,4,3,2,0:T(8,128)(2,1)} %convolution_convert_fusion.5), kind=kOutput, calls=%fused_computation.733 | convolution fusion | flops 1660944896 | bytes 56723456 | tf_op jit(solution)/shard_map/sub | solution.py:30
  427.1 22.1 %convert_reduce_fusion.7 = (f32[4,512]{1,0:T(4,128)S(1)}, bf16[4,512,768]{2,1,0:T(8,128)(2,1)S(1)}) fusion(f32[768]{0:T(1024)S(1)} %copy-done.144, bf16[4,512,2,6,64]{1,4,3,2,0:T(8,128)(2,1)} %add_convert_fusion.11, bf16[16,2,512,768]{3,2,1,0:T(8,128)(2,1)} %bitcast.736, s32[]{:T(128)S(6)} %add.1104, s32[]{:T(128)S(6)} %select_n.440, ...), kind=kOutput, calls=%fused_computation.172 | convolution fusion | flops 4062705664 | bytes 61058056 | tf_op jit(solution)/shard_map/rqthk,thkd->rqd/dot_general | solution.py:32
  451.0 25.5 %convert_reduce_fusion.6 = (f32[4,512]{1,0:T(4,128)S(1)}, bf16[4,512,768]{2,1,0:T(8,128)(2,1)S(1)}) fusion(f32[768]{0:T(1024)S(1)} %copy-done.193, bf16[2,1536,768,1]{2,1,0,3:T(8,128)(2,1)} %bitcast.836, bf16[2,768,1536,1]{2,1,0,3:T(8,128)(2,1)} %bitcast.832, f32[2,1536]{1,0:T(2,128)S(1)} %copy-done.105, bf16[4,512,768]{2,1,0:T(8,128)(2,1)} %copy-done.21, ...), kind=kOutput, calls=%fused_computation.169 | convolution fusion | flops 19365099520 | bytes 15774720 | tf_op jit(solution)/shard_map/rstf,tfd->rsd/dot_general | solution.py:39
  477.6 5.7 convolution_convert_fusion.4
  492.7 6.6 add_convert_fusion.14
  504.2 6.5 add_convert_fusion.15
  510.6 26.4 %fusion.513 = (f32[4,2,6,512]{3,2,1,0:T(8,128)S(1)}, f32[4,2,6,512,512]{3,4,2,1,0:T(8,128)}) fusion(pred[4,512]{1,0:T(4,128)(4,1)S(1)} %copy-done.161, bf16[4,512,2,6,64]{1,4,3,2,0:T(8,128)(2,1)} %add_convert_fusion.14, bf16[4,512,2,6,64]{1,4,3,2,0:T(8,128)(2,1)S(1)} %convolution_convert_fusion.7), kind=kOutput, calls=%fused_computation.731 | convolution fusion | flops 1660944896 | bytes 56723456 | tf_op jit(solution)/shard_map/sub | solution.py:30
  537.0 22.1 %convert_reduce_fusion.10 = (f32[4,512]{1,0:T(4,128)S(1)}, bf16[4,512,768]{2,1,0:T(8,128)(2,1)S(1)}) fusion(f32[768]{0:T(1024)S(1)} %copy-done.144, bf16[4,512,2,6,64]{1,4,3,2,0:T(8,128)(2,1)} %add_convert_fusion.15, bf16[16,2,512,768]{3,2,1,0:T(8,128)(2,1)} %bitcast.740, s32[]{:T(128)S(6)} %select_n.440, f32[4,2,6,512,512]{3,4,2,1,0:T(8,128)} %get-tuple-element.518, ...), kind=kOutput, calls=%fused_computation.181 | convolution fusion | flops 4062705664 | bytes 61058052 | tf_op jit(solution)/shard_map/rqthk,thkd->rqd/dot_general | solution.py:32
  560.9 25.5 %convert_reduce_fusion.9 = (f32[4,512]{1,0:T(4,128)S(1)}, bf16[4,512,768]{2,1,0:T(8,128)(2,1)S(1)}) fusion(f32[768]{0:T(1024)S(1)} %copy-done.193, bf16[2,1536,768,1]{2,1,0,3:T(8,128)(2,1)} %bitcast.837, bf16[2,768,1536,1]{2,1,0,3:T(8,128)(2,1)} %bitcast.833, f32[2,1536]{1,0:T(2,128)S(1)} %copy-done.105, bf16[4,512,768]{2,1,0:T(8,128)(2,1)} %copy-done.18, ...), kind=kOutput, calls=%fused_computation.178 | convolution fusion | flops 19365099520 | bytes 15774720 | tf_op jit(solution)/shard_map/rstf,tfd->rsd/dot_general | solution.py:39
  587.4 5.8 convolution_convert_fusion.6
  597.9 6.7 add_convert_fusion.13
  605.9 25.7 %fusion.544 = (f32[4,2,6,512]{3,2,1,0:T(8,128)S(1)}, f32[4,2,6,512,512]{3,4,2,1,0:T(8,128)}) fusion(pred[4,512]{1,0:T(4,128)(4,1)S(1)} %copy-done.168, bf16[4,512,2,6,64]{1,4,3,2,0:T(8,128)(2,1)} %add_convert_fusion, bf16[4,512,2,6,64]{1,4,3,2,0:T(8,128)(2,1)} %convolution_convert_fusion), kind=kOutput, calls=%fused_computation.738 | convolution fusion | flops 1660944896 | bytes 56723456 | tf_op jit(solution)/shard_map/sub | solution.py:30
  631.6 22.1 %convert_reduce_fusion.12 = (f32[4,512]{1,0:T(4,128)S(1)}, bf16[4,512,768]{2,1,0:T(8,128)(2,1)S(1)}) fusion(f32[768]{0:T(1024)S(1)} %copy-done.142, bf16[4,512,2,6,64]{1,4,3,2,0:T(8,128)(2,1)} %add_convert_fusion.1, bf16[4,512,768]{2,1,0:T(8,128)(2,1)} %copy-done.12, f32[4,2,6,512,512]{3,4,2,1,0:T(8,128)} %get-tuple-element.548, ...), kind=kOutput, calls=%fused_computation.194 | convolution fusion | flops 4062705664 | bytes 61058048 | tf_op jit(solution)/shard_map/rqthk,thkd->rqd/dot_general | solution.py:32
  656.1 25.9 %fusion.536 = (f32[4,2,6,512]{3,2,1,0:T(8,128)S(1)}, f32[4,2,6,512,512]{3,4,2,1,0:T(8,128)}) fusion(pred[4,512]{1,0:T(4,128)(4,1)S(1)} %copy-done.166, bf16[4,512,2,6,64]{1,4,3,2,0:T(8,128)(2,1)} %add_convert_fusion.4, bf16[4,512,2,6,64]{1,4,3,2,0:T(8,128)(2,1)} %convolution_convert_fusion.2), kind=kOutput, calls=%fused_computation.736 | convolution fusion | flops 1660944896 | bytes 56723456 | tf_op jit(solution)/shard_map/sub | solution.py:30
  682.0 22.1 %convert_reduce_fusion.13 = (f32[4,512]{1,0:T(4,128)S(1)}, bf16[4,512,768]{2,1,0:T(8,128)(2,1)S(1)}) fusion(f32[768]{0:T(1024)S(1)} %copy-done.142, bf16[4,512,2,6,64]{1,4,3,2,0:T(8,128)(2,1)} %add_convert_fusion.5, bf16[4,512,768]{2,1,0:T(8,128)(2,1)} %get-tuple-element.538, f32[4,2,6,512,512]{3,4,2,1,0:T(8,128)} %get-tuple-element.540, ...), kind=kOutput, calls=%fused_computation.196 | convolution fusion | flops 4062705664 | bytes 61058048 | tf_op jit(solution)/shard_map/rqthk,thkd->rqd/dot_general | solution.py:32
  706.5 26.1 %fusion.528 = (f32[4,2,6,512]{3,2,1,0:T(8,128)S(1)}, f32[4,2,6,512,512]{3,4,2,1,0:T(8,128)}) fusion(pred[4,512]{1,0:T(4,128)(4,1)S(1)} %copy-done.164, bf16[4,512,2,6,64]{1,4,3,2,0:T(8,128)(2,1)} %add_convert_fusion.8, bf16[4,512,2,6,64]{1,4,3,2,0:T(8,128)(2,1)} %convolution_convert_fusion.4), kind=kOutput, calls=%fused_computation.734 | convolution fusion | flops 1660944896 | bytes 56723456 | tf_op jit(solution)/shard_map/sub | solution.py:30
  732.6 22.1 %convert_reduce_fusion.14 = (f32[4,512]{1,0:T(4,128)S(1)}, bf16[4,512,768]{2,1,0:T(8,128)(2,1)S(1)}) fusion(f32[768]{0:T(1024)S(1)} %copy-done.142, bf16[4,512,2,6,64]{1,4,3,2,0:T(8,128)(2,1)} %add_convert_fusion.9, bf16[4,512,768]{2,1,0:T(8,128)(2,1)} %copy-done.16, f32[4,2,6,512,512]{3,4,2,1,0:T(8,128)} %get-tuple-element.532, ...), kind=kOutput, calls=%fused_computation.198 | convolution fusion | flops 4062705664 | bytes 61058048 | tf_op jit(solution)/shard_map/rqthk,thkd->rqd/dot_general | solution.py:32
  755.9 25.9 %fusion.520 = (f32[4,2,6,512]{3,2,1,0:T(8,128)S(1)}, f32[4,2,6,512,512]{3,4,2,1,0:T(8,128)}) fusion(pred[4,512]{1,0:T(4,128)(4,1)S(1)} %copy-done.162, bf16[4,512,2,6,64]{1,4,3,2,0:T(8,128)(2,1)} %add_convert_fusion.12, bf16[4,512,2,6,64]{1,4,3,2,0:T(8,128)(2,1)} %convolution_convert_fusion.6), kind=kOutput, calls=%fused_computation.732 | convolution fusion | flops 1660944896 | bytes 56723456 | tf_op jit(solution)/shard_map/sub | solution.py:30
  781.8 23.9 %convert_reduce_fusion.15 = (f32[4,512]{1,0:T(4,128)S(1)}, bf16[4,512,768]{2,1,0:T(8,128)(2,1)}) fusion(f32[768]{0:T(1024)S(1)} %copy-done.142, bf16[4,512,2,6,64]{1,4,3,2,0:T(8,128)(2,1)} %add_convert_fusion.13, bf16[4,512,768]{2,1,0:T(8,128)(2,1)} %copy-done.17, f32[4,2,6,512,512]{3,4,2,1,0:T(8,128)} %get-tuple-element.524, ...), kind=kOutput, calls=%fused_computation.200 | convolution fusion | flops 4062705664 | bytes 61058048 | tf_op jit(solution)/shard_map/rqthk,thkd->rqd/dot_general | solution.py:32
  808.9 11.7 fusion.145
  824.8 60.6 %scatter_custom_fusion = s32[32768]{0:T(1024)S(1)} fusion(s32[16384]{0:T(1024)S(1)} %bitcast.808, s32[16384]{0:T(1024)} %pad_add_fusion, s32[]{:T(128)} %constant.330.clone.1), kind=kCustom, calls=%fused_computation.479 | custom fusion | bytes 131584 | tf_op jit(solution)/shard_map/scatter | solution.py:190
  892.6 64.4 %collective-permute-done.16 = bf16[2048,768]{1,0:T(8,128)(2,1)} collective-permute-done((bf16[2048,768]{1,0:T(8,128)(2,1)}, bf16[2048,768]{1,0:T(8,128)(2,1)}, u32[]{:S(2)}, u32[]{:S(2)}) %collective-permute-start.16) | collective-permute-done | bytes 3145760 | tf_op jit(solution)/shard_map/ppermute | solution.py:211
  963.7 60.7 %collective-permute-done.17 = bf16[2048,768]{1,0:T(8,128)(2,1)} collective-permute-done((bf16[2048,768]{1,0:T(8,128)(2,1)}, bf16[2048,768]{1,0:T(8,128)(2,1)}, u32[]{:S(2)}, u32[]{:S(2)}) %collective-permute-start.17) | collective-permute-done | bytes 3145760 | tf_op jit(solution)/shard_map/ppermute | solution.py:211
  1027.4 9.8 pad_maximum_fusion.3
  1037.2 54.4 %collective-permute-done.18 = bf16[2048,768]{1,0:T(8,128)(2,1)S(1)} collective-permute-done((bf16[2048,768]{1,0:T(8,128)(2,1)}, bf16[2048,768]{1,0:T(8,128)(2,1)S(1)}, u32[]{:S(2)}, u32[]{:S(2)}) %collective-permute-start.18) | collective-permute-done | bytes 3145760 | tf_op jit(solution)/shard_map/ppermute | solution.py:211
  1098.7 9.6 pad_maximum_fusion.5
  1108.6 5.8 pad_maximum_fusion.4
  1121.7 487.3 %conditional.2 = (bf16[8192,768]{1,0:T(8,128)(2,1)}) conditional(s32[]{:T(128)} %clamp.27, (bf16[2048,768]{1,0:T(8,128)(2,1)}, bf16[2048,768]{1,0:T(8,128)(2,1)}, bf16[2048,768]{1,0:T(8,128)(2,1)}, bf16[2048,768]{1,0:T(8,128)(2,1)}, pred[8192]{0:T(1024)(128)(4,1)S(1)}, /*index=5*/f32[8192]{0:T(1024)}, s32[8192]{0:T(1024)S(1)}, ...), branch_computations={%region_92.93_spmd, %region_93.94_spmd, %region_94.95_spmd} | conditional | flops 309546188800 | bytes 568624640
  1123.1 21.2 %gather_fusion.1 = bf16[3072,768]{1,0:T(8,128)(2,1)} fusion(bf16[8192,768]{1,0:T(8,128)(2,1)} %get-tuple-element.297, s32[3072]{0:T(1024)S(1)} %fusion.3), kind=kCustom, calls=%fused_computation.1 | custom fusion | bytes 9449472 | tf_op jit(solution)/shard_map/cond/branch_0_fun/gather | solution.py:228
  1144.2 43.5 %branch_0_fun.5 = bf16[3072,768]{1,0:T(8,128)(2,1)} custom-call(s32[36]{0:T(128)S(1)} %get-tuple-element.292.visit_tile, s32[36]{0:T(128)S(1)} %get-tuple-element.293.visit_expert, s32[36]{0:T(128)S(1)} %get-tuple-element.294.visit_lo, s32[36]{0:T(128)S(1)} %get-tuple-element.295.visit_hi, s32[1]{0:T(128)} %get-tuple-element.296.n_visits, ...), custom_call_target="tpu_custom_call" | custom-call | flops 28991029248 | bytes 9437184 | tf_op jit(solution)/shard_map/cond/branch_0_fun/pallas_call | solution.py:88
  1187.7 5.9 collective-permute-start
  1193.6 20.8 %gather_fusion.2 = bf16[3072,768]{1,0:T(8,128)(2,1)} fusion(bf16[8192,768]{1,0:T(8,128)(2,1)} %get-tuple-element.304, s32[3072]{0:T(1024)S(1)} %fusion.4), kind=kCustom, calls=%fused_computation.2 | custom fusion | bytes 9449472 | tf_op jit(solution)/shard_map/cond/branch_0_fun/gather | solution.py:228
  1214.4 43.5 %branch_0_fun.6 = bf16[3072,768]{1,0:T(8,128)(2,1)} custom-call(s32[36]{0:T(128)S(1)} %get-tuple-element.299.visit_tile, s32[36]{0:T(128)S(1)} %get-tuple-element.300.visit_expert, s32[36]{0:T(128)S(1)} %get-tuple-element.301.visit_lo, s32[36]{0:T(128)S(1)} %get-tuple-element.302.visit_hi, s32[1]{0:T(128)} %get-tuple-element.303.n_visits, ...), custom_call_target="tpu_custom_call" | custom-call | flops 28991029248 | bytes 9437184 | tf_op jit(solution)/shard_map/cond/branch_0_fun/pallas_call | solution.py:88
  1257.8 20.8 %gather_fusion.3 = bf16[3072,768]{1,0:T(8,128)(2,1)} fusion(bf16[8192,768]{1,0:T(8,128)(2,1)} %get-tuple-element.311, s32[3072]{0:T(1024)S(1)} %fusion.5), kind=kCustom, calls=%fused_computation.3 | custom fusion | bytes 9449472 | tf_op jit(solution)/shard_map/cond/branch_0_fun/gather | solution.py:228
  1278.6 43.6 %branch_0_fun.7 = bf16[3072,768]{1,0:T(8,128)(2,1)} custom-call(s32[36]{0:T(128)S(1)} %get-tuple-element.306.visit_tile, s32[36]{0:T(128)S(1)} %get-tuple-element.307.visit_expert, s32[36]{0:T(128)S(1)} %get-tuple-element.308.visit_lo, s32[36]{0:T(128)S(1)} %get-tuple-element.309.visit_hi, s32[1]{0:T(128)} %get-tuple-element.310.n_visits, ...), custom_call_target="tpu_custom_call" | custom-call | flops 28991029248 | bytes 9437184 | tf_op jit(solution)/shard_map/cond/branch_0_fun/pallas_call | solution.py:88
  1326.6 20.8 %gather_fusion = bf16[3072,768]{1,0:T(8,128)(2,1)} fusion(bf16[8192,768]{1,0:T(8,128)(2,1)} %get-tuple-element.286, s32[3072]{0:T(1024)S(1)} %fusion.2), kind=kCustom, calls=%fused_computation | custom fusion | bytes 9449472 | tf_op jit(solution)/shard_map/cond/branch_0_fun/gather | solution.py:228
  1348.2 43.6 %branch_0_fun.4 = bf16[3072,768]{1,0:T(8,128)(2,1)} custom-call(s32[36]{0:T(128)} %get-tuple-element.281.visit_tile, s32[36]{0:T(128)S(1)} %get-tuple-element.282.visit_expert, s32[36]{0:T(128)S(1)} %get-tuple-element.283.visit_lo, s32[36]{0:T(128)S(1)} %get-tuple-element.284.visit_hi, s32[1]{0:T(128)} %get-tuple-element.285.n_visits, ...), custom_call_target="tpu_custom_call" | custom-call | flops 28991029248 | bytes 9437184 | tf_op jit(solution)/shard_map/cond/branch_0_fun/pallas_call | solution.py:88
  1391.8 70.7 %collective-permute-done.2 = bf16[3072,768]{1,0:T(8,128)(2,1)} collective-permute-done((bf16[3072,768]{1,0:T(8,128)(2,1)}, bf16[3072,768]{1,0:T(8,128)(2,1)}, u32[]{:S(2)}, u32[]{:S(2)}) %collective-permute-start.2) | collective-permute-done | bytes 4718624 | tf_op jit(solution)/shard_map/cond/branch_0_fun/ppermute | solution.py:230
  1462.5 23.4 %pad_maximum_fusion = bf16[12288,768]{1,0:T(8,128)(2,1)} fusion(bf16[3072,768]{1,0:T(8,128)(2,1)} %collective-permute-done.2, bf16[3072,768]{1,0:T(8,128)(2,1)} %collective-permute-done.1, bf16[3072,768]{1,0:T(8,128)(2,1)} %collective-permute-done, bf16[3072,768]{1,0:T(8,128)(2,1)} %branch_0_fun.4), kind=kLoop, calls=%fused_computation.20 | loop fusion | flops 75497472 | bytes 37748736 | tf_op jit(solution)/shard_map/cond/branch_0_fun/concatenate | solution.py:231
  1485.9 46.0 %gather_fusion.4 = bf16[8192,768]{1,0:T(8,128)(2,1)} fusion(bf16[12288,768]{1,0:T(8,128)(2,1)} %pad_maximum_fusion, s32[8192]{0:T(1024)S(1)} %get-tuple-element.459), kind=kCustom, calls=%fused_computation.4 | custom fusion | bytes 25198592 | tf_op jit(solution)/shard_map/cond/branch_0_fun/gather | solution.py:232
  1532.0 46.1 %gather_fusion.5 = bf16[8192,768]{1,0:T(8,128)(2,1)} fusion(bf16[12288,768]{1,0:T(8,128)(2,1)} %pad_maximum_fusion, s32[8192]{0:T(1024)S(1)} %get-tuple-element.460), kind=kCustom, calls=%fused_computation.5 | custom fusion | bytes 25198592 | tf_op jit(solution)/shard_map/cond/branch_0_fun/gather | solution.py:233
  1578.1 22.6 %add_add_fusion = bf16[8192,768]{1,0:T(8,128)(2,1)} fusion(bf16[8192,768]{1,0:T(8,128)(2,1)} %gather_fusion.5, bf16[8192,768]{1,0:T(8,128)(2,1)} %gather_fusion.4, bf16[2048,768]{1,0:T(8,128)(2,1)S(1)} %copy-done.4, bf16[2048,768]{1,0:T(8,128)(2,1)} %get-tuple-element.277, bf16[2048,768]{1,0:T(8,128)(2,1)} %get-tuple-element.276, ...), kind=kLoop, calls=%fused_computation.19 | loop fusion | flops 106954752 | bytes 50413568 | tf_op jit(solution)/shard_map/cond/branch_0_fun/add | solution.py:235
  1609.0 294.9 %all-gather.17.cloned.1.call-done = bf16[16,2,512,768]{3,2,1,0:T(8,128)(2,1)} async-done(((bf16[16,1,512,768]{3,2,1,0:T(8,128)(2,1)}), bf16[16,2,512,768]{3,2,1,0:T(8,128)(2,1)}) %all-gather.17.cloned.1.call-update) | async-done | bytes 25165840 | tf_op jit(solution)/shard_map/all_gather | solution.py:241
  1903.9 20.5 %copy.739 = bf16[32,512,768]{2,1,0:T(8,128)(2,1)} copy(bf16[32,512,768]{2,1,0:T(8,128)(2,1)} %bitcast.722) | data formatting | bytes 50331648
  (577 shorter events, 199.0 us)
Async XLA Ops:
  6.5 951.5 %copy-start = (f32[768,16]{0,1:T(8,128)S(1)}, f32[768,16]{0,1:T(8,128)}, u32[]{:S(2)}) copy-start(f32[768,16]{0,1:T(8,128)} %param.40) | copy-start | bytes 147460
  6.5 92.3 %all-gather.19.cloned.1.call-start = ((), (), s32[]{:S(2)}) async-start(), calls=%async_computation.1 | async-start | bytes 7077888 | tf_op jit(solution)/shard_map/all_gather | solution.py:142
  17.2 182.7 %all-gather.21.cloned.1.call-start = ((), (), s32[]{:S(2)}) async-start(), calls=%async_computation.2 | async-start | bytes 7077888 | tf_op jit(solution)/shard_map/all_gather | solution.py:147
  18.0 183.7 %all-gather.23.cloned.1.call-start = ((), (), s32[]{:S(2)}) async-start(), calls=%async_computation.3 | async-start | bytes 7077888 | tf_op jit(solution)/shard_map/all_gather | solution.py:148
  18.7 244.5 %all-gather.25.cloned.1.call-start = ((), (), s32[]{:S(2)}) async-start(), calls=%async_computation.4 | async-start | bytes 7077888 | tf_op jit(solution)/shard_map/all_gather | solution.py:142
  23.4 1098.3 %all-gather.27.cloned.1.call-start = ((), (), s32[]{:S(2)}) async-start(), calls=%async_computation.5 | async-start | bytes 28311552 | tf_op jit(solution)/shard_map/all_gather | solution.py:150
  24.0 1097.7 %all-gather.29.cloned.1.call-start = ((), (), s32[]{:S(2)}) async-start(), calls=%async_computation.6 | async-start | bytes 28311552 | tf_op jit(solution)/shard_map/all_gather | solution.py:151
  24.6 1879.3 %all-gather.17.cloned.1.call-start = ((), (), s32[]{:S(2)}) async-start(), calls=%async_computation | async-start | bytes 37748736 | tf_op jit(solution)/shard_map/all_gather | solution.py:241
  41.8 36.4 %copy-start.159 = (s32[1,1,4]{2,1,0:T(1,128)}, s32[1,1,4]{2,1,0:T(1,128)S(1)}, u32[]{:S(2)}) copy-start(s32[1,1,4]{2,1,0:T(1,128)S(1)} %get-tuple-element.500) | copy-start | bytes 52
  73.3 48.1 %copy-start.116 = (f32[2,6,64]{2,1,0:T(8,128)}, f32[2,6,64]{2,1,0:T(8,128)S(1)}, u32[]{:S(2)}) copy-start(f32[2,6,64]{2,1,0:T(8,128)S(1)} %get-tuple-element.494) | copy-start | bytes 9220
  95.2 47.7 %copy-start.136 = (f32[768]{0:T(1024)}, f32[768]{0:T(1024)S(1)}, u32[]{:S(2)}) copy-start(f32[768]{0:T(1024)S(1)} %get-tuple-element.429) | copy-start | bytes 9220
  95.2 47.7 %copy-start.139 = (f32[768]{0:T(1024)}, f32[768]{0:T(1024)S(1)}, u32[]{:S(2)}) copy-start(f32[768]{0:T(1024)S(1)} %get-tuple-element.572) | copy-start | bytes 9220
  95.2 225.0 %copy-start.132 = (f32[768]{0:T(1024)}, f32[768]{0:T(1024)S(1)}, u32[]{:S(2)}) copy-start(f32[768]{0:T(1024)S(1)} %get-tuple-element.428) | copy-start | bytes 9220
  95.2 225.0 %copy-start.134 = (f32[768]{0:T(1024)}, f32[768]{0:T(1024)S(1)}, u32[]{:S(2)}) copy-start(f32[768]{0:T(1024)S(1)} %get-tuple-element.573) | copy-start | bytes 9220
  226.9 36.3 %copy-start.12 = (bf16[4,512,768]{2,1,0:T(8,128)(2,1)}, bf16[4,512,768]{2,1,0:T(8,128)(2,1)S(1)}, u32[]{:S(2)}) copy-start(bf16[4,512,768]{2,1,0:T(8,128)(2,1)S(1)} %get-tuple-element.546) | copy-start | bytes 9437188
  320.1 29.8 %copy-start.13 = (bf16[4,512,768]{2,1,0:T(8,128)(2,1)S(1)}, bf16[4,512,768]{2,1,0:T(8,128)(2,1)}, u32[]{:S(2)}) copy-start(bf16[4,512,768]{2,1,0:T(8,128)(2,1)} %copy-done.12) | copy-start | bytes 9437188
  320.2 29.8 %copy-start.91 = (f32[4,512]{1,0:T(4,128)S(1)}, f32[4,512]{1,0:T(4,128)}, u32[]{:S(2)}) copy-start(f32[4,512]{1,0:T(4,128)} %copy-done.90) | copy-start | bytes 24580
  320.2 29.8 %copy-start.109 = (f32[4,512]{1,0:T(4,128)S(1)}, f32[4,512]{1,0:T(4,128)}, u32[]{:S(2)}) copy-start(f32[4,512]{1,0:T(4,128)} %add_rsqrt_fusion.4) | copy-start | bytes 24580
  320.2 29.8 %copy-start.126 = (f32[768]{0:T(1024)S(1)}, f32[768]{0:T(1024)}, u32[]{:S(2)}) copy-start(f32[768]{0:T(1024)} %get-tuple-element.430) | copy-start | bytes 9220
  320.2 29.8 %copy-start.129 = (f32[768]{0:T(1024)S(1)}, f32[768]{0:T(1024)}, u32[]{:S(2)}) copy-start(f32[768]{0:T(1024)} %get-tuple-element.571) | copy-start | bytes 9220
  653.7 28.3 %copy-start.2 = (bf16[4,512,768]{2,1,0:T(8,128)(2,1)}, bf16[4,512,768]{2,1,0:T(8,128)(2,1)S(1)}, u32[]{:S(2)}) copy-start(bf16[4,512,768]{2,1,0:T(8,128)(2,1)S(1)} %get-tuple-element.556) | copy-start | bytes 9437188
  704.2 28.5 %copy-start.7 = (bf16[4,512,768]{2,1,0:T(8,128)(2,1)}, bf16[4,512,768]{2,1,0:T(8,128)(2,1)S(1)}, u32[]{:S(2)}) copy-start(bf16[4,512,768]{2,1,0:T(8,128)(2,1)S(1)} %get-tuple-element.554) | copy-start | bytes 9437188
  754.8 27.0 %copy-start.8 = (bf16[4,512,768]{2,1,0:T(8,128)(2,1)}, bf16[4,512,768]{2,1,0:T(8,128)(2,1)S(1)}, u32[]{:S(2)}) copy-start(bf16[4,512,768]{2,1,0:T(8,128)(2,1)S(1)} %get-tuple-element.552) | copy-start | bytes 9437188
  808.8 76.6 %copy-start.146 = (s32[4,1]{0,1:T(1,128)S(1)}, s32[4,1]{0,1:T(1,128)}, u32[]{:S(2)}) copy-start(s32[4,1]{0,1:T(1,128)} %copy-done.145) | copy-start | bytes 52
  808.8 76.6 %copy-start.147 = (s32[4]{0:T(128)S(1)}, s32[4]{0:T(128)}, u32[]{:S(2)}) copy-start(s32[4]{0:T(128)} %get-tuple-element.509) | copy-start | bytes 52
  808.8 76.6 %copy-start.148 = (s32[4]{0:T(128)S(1)}, s32[4]{0:T(128)}, u32[]{:S(2)}) copy-start(s32[4]{0:T(128)} %get-tuple-element.510) | copy-start | bytes 52
  808.8 76.6 %copy-start.150 = (s32[4,1]{0,1:T(1,128)S(1)}, s32[4,1]{0,1:T(1,128)}, u32[]{:S(2)}) copy-start(s32[4,1]{0,1:T(1,128)} %copy-done.149) | copy-start | bytes 52
  808.8 76.6 %copy-start.151 = (s32[4]{0:T(128)S(1)}, s32[4]{0:T(128)}, u32[]{:S(2)}) copy-start(s32[4]{0:T(128)} %get-tuple-element.511) | copy-start | bytes 52
  808.8 76.6 %copy-start.152 = (s32[4]{0:T(128)S(1)}, s32[4]{0:T(128)}, u32[]{:S(2)}) copy-start(s32[4]{0:T(128)} %get-tuple-element.512) | copy-start | bytes 52
  808.8 76.6 %copy-start.169 = (s32[36]{0:T(128)S(1)}, s32[36]{0:T(128)}, u32[]{:S(2)}) copy-start(s32[36]{0:T(128)} %broadcast_minimum_fusion) | copy-start | bytes 436
  808.9 76.6 %copy-start.172 = (s32[36]{0:T(128)S(1)}, s32[36]{0:T(128)}, u32[]{:S(2)}) copy-start(s32[36]{0:T(128)} %broadcast_minimum_fusion.1) | copy-start | bytes 436
  808.9 76.7 %copy-start.158 = (s32[4,1]{0,1:T(1,128)S(1)}, s32[4,1]{0,1:T(1,128)}, u32[]{:S(2)}) copy-start(s32[4,1]{0,1:T(1,128)} %copy-done.157) | copy-start | bytes 52
  808.9 76.7 %copy-start.160 = (s32[1,1,4]{2,1,0:T(1,128)S(1)}, s32[1,1,4]{2,1,0:T(1,128)}, u32[]{:S(2)}) copy-start(s32[1,1,4]{2,1,0:T(1,128)} %copy-done.159) | copy-start | bytes 52
  808.9 76.7 %copy-start.180 = (s32[4,1]{0,1:T(1,128)S(1)}, s32[4,1]{0,1:T(1,128)}, u32[]{:S(2)}) copy-start(s32[4,1]{0,1:T(1,128)} %copy-done.178) | copy-start | bytes 52
  808.9 76.8 %copy-start.154 = (s32[4,1]{0,1:T(1,128)S(1)}, s32[4,1]{0,1:T(1,128)}, u32[]{:S(2)}) copy-start(s32[4,1]{0,1:T(1,128)} %copy-done.153) | copy-start | bytes 52
  808.9 76.8 %copy-start.155 = (s32[4]{0:T(128)S(1)}, s32[4]{0:T(128)}, u32[]{:S(2)}) copy-start(s32[4]{0:T(128)} %get-tuple-element.513) | copy-start | bytes 52
  808.9 76.8 %copy-start.156 = (s32[4]{0:T(128)S(1)}, s32[4]{0:T(128)}, u32[]{:S(2)}) copy-start(s32[4]{0:T(128)} %get-tuple-element.514) | copy-start | bytes 52
  808.9 76.8 %copy-start.173 = (s32[36]{0:T(128)S(1)}, s32[36]{0:T(128)}, u32[]{:S(2)}) copy-start(s32[36]{0:T(128)} %broadcast_minimum_fusion.2) | copy-start | bytes 436
  820.7 203.7 %copy-start.9 = (bf16[4,512,768]{2,1,0:T(8,128)(2,1)S(1)}, bf16[4,512,768]{2,1,0:T(8,128)(2,1)}, u32[]{:S(2)}) copy-start(bf16[4,512,768]{2,1,0:T(8,128)(2,1)} %get-tuple-element.504) | copy-start | bytes 9437188
  820.7 68.8 %collective-permute-start.15 = (bf16[2048,768]{1,0:T(8,128)(2,1)}, bf16[2048,768]{1,0:T(8,128)(2,1)}, u32[]{:S(2)}, u32[]{:S(2)}) collective-permute-start(bf16[2048,768]{1,0:T(8,128)(2,1)} %bitcast.564), channel_id=1, source_target_pairs={{0,2},{1,3},{2,0},{3,1},{4,6},{5,7},{6,4},{7,5}} | collective-permute-start | bytes 9437192 | tf_op jit(solution)/shard_map/ppermute | solution.py:211
  821.0 135.9 %collective-permute-start.16 = (bf16[2048,768]{1,0:T(8,128)(2,1)}, bf16[2048,768]{1,0:T(8,128)(2,1)}, u32[]{:S(2)}, u32[]{:S(2)}) collective-permute-start(bf16[2048,768]{1,0:T(8,128)(2,1)} %bitcast.563), channel_id=1, source_target_pairs={{0,2},{1,3},{2,0},{3,1},{4,6},{5,7},{6,4},{7,5}} | collective-permute-start | bytes 9437192 | tf_op jit(solution)/shard_map/ppermute | solution.py:211
  822.2 202.1 %collective-permute-start.17 = (bf16[2048,768]{1,0:T(8,128)(2,1)}, bf16[2048,768]{1,0:T(8,128)(2,1)}, u32[]{:S(2)}, u32[]{:S(2)}) collective-permute-start(bf16[2048,768]{1,0:T(8,128)(2,1)} %bitcast.562), channel_id=1, source_target_pairs={{0,2},{1,3},{2,0},{3,1},{4,6},{5,7},{6,4},{7,5}} | collective-permute-start | bytes 9437192 | tf_op jit(solution)/shard_map/ppermute | solution.py:211
  885.8 207.6 %collective-permute-start.10 = (bf16[2048,768]{1,0:T(8,128)(2,1)}, bf16[2048,768]{1,0:T(8,128)(2,1)S(1)}, u32[]{:S(2)}, u32[]{:S(2)}) collective-permute-start(bf16[2048,768]{1,0:T(8,128)(2,1)} %bitcast.564), channel_id=1, source_target_pairs={{0,1},{1,0},{2,3},{3,2},{4,5},{5,4},{6,7},{7,6}} | collective-permute-start | bytes 9437192 | tf_op jit(solution)/shard_map/ppermute | solution.py:213
  887.4 206.1 %collective-permute-start.11 = (bf16[2048,768]{1,0:T(8,128)(2,1)}, bf16[2048,768]{1,0:T(8,128)(2,1)S(1)}, u32[]{:S(2)}, u32[]{:S(2)}) collective-permute-start(bf16[2048,768]{1,0:T(8,128)(2,1)} %bitcast.563), channel_id=1, source_target_pairs={{0,1},{1,0},{2,3},{3,2},{4,5},{5,4},{6,7},{7,6}} | collective-permute-start | bytes 9437192 | tf_op jit(solution)/shard_map/ppermute | solution.py:213
  889.5 204.4 %collective-permute-start.12 = (bf16[2048,768]{1,0:T(8,128)(2,1)}, bf16[2048,768]{1,0:T(8,128)(2,1)S(1)}, u32[]{:S(2)}, u32[]{:S(2)}) collective-permute-start(bf16[2048,768]{1,0:T(8,128)(2,1)} %bitcast.562), channel_id=1, source_target_pairs={{0,1},{1,0},{2,3},{3,2},{4,5},{5,4},{6,7},{7,6}} | collective-permute-start | bytes 9437192 | tf_op jit(solution)/shard_map/ppermute | solution.py:213
  956.9 134.7 %collective-permute-start.18 = (bf16[2048,768]{1,0:T(8,128)(2,1)}, bf16[2048,768]{1,0:T(8,128)(2,1)S(1)}, u32[]{:S(2)}, u32[]{:S(2)}) collective-permute-start(bf16[2048,768]{1,0:T(8,128)(2,1)} %bitcast.718), channel_id=1, source_target_pairs={{0,2},{1,3},{2,0},{3,1},{4,6},{5,7},{6,4},{7,5}} | collective-permute-start | bytes 9437192 | tf_op jit(solution)/shard_map/ppermute | solution.py:211
  1024.4 83.9 %collective-permute-start.13 = (bf16[2048,768]{1,0:T(8,128)(2,1)S(1)}, bf16[2048,768]{1,0:T(8,128)(2,1)S(1)}, u32[]{:S(2)}, u32[]{:S(2)}) collective-permute-start(bf16[2048,768]{1,0:T(8,128)(2,1)S(1)} %bitcast.719), channel_id=1, source_target_pairs={{0,1},{1,0},{2,3},{3,2},{4,5},{5,4},{6,7},{7,6}} | collective-permute-start | bytes 9437192 | tf_op jit(solution)/shard_map/ppermute | solution.py:213
  1037.2 60.5 %copy-start.74 = (s32[16,1,512]{2,1,0:T(1,128)S(1)}, s32[16,1,512]{2,1,0:T(1,128)}, u32[]{:S(2)}) copy-start(s32[16,1,512]{2,1,0:T(1,128)} %copy-done.73) | copy-start | bytes 98308
  1037.2 60.5 %copy-start.76 = (s32[16,1,512]{2,1,0:T(1,128)S(1)}, s32[16,1,512]{2,1,0:T(1,128)}, u32[]{:S(2)}) copy-start(s32[16,1,512]{2,1,0:T(1,128)} %copy-done.75) | copy-start | bytes 98308
  1037.2 60.8 %copy-start.48 = (pred[2,4,8,128]{3,1,2,0:T(4,128)(4,1)S(1)}, pred[2,4,8,128]{3,1,2,0:T(4,128)(4,1)}, u32[]{:S(2)}) copy-start(pred[2,4,8,128]{3,1,2,0:T(4,128)(4,1)} %copy-done.47) | copy-start | bytes 24580
  1037.2 60.8 %copy-start.56 = (pred[2,4,8,128]{3,1,2,0:T(4,128)(4,1)S(1)}, pred[2,4,8,128]{3,1,2,0:T(4,128)(4,1)}, u32[]{:S(2)}) copy-start(pred[2,4,8,128]{3,1,2,0:T(4,128)(4,1)} %copy-done.55) | copy-start | bytes 24580
  1091.7 22.7 %collective-permute-start.20 = (bf16[2048,768]{1,0:T(8,128)(2,1)}, bf16[2048,768]{1,0:T(8,128)(2,1)S(1)}, u32[]{:S(2)}, u32[]{:S(2)}) collective-permute-start(bf16[2048,768]{1,0:T(8,128)(2,1)} %collective-permute-done.15), channel_id=1, source_target_pairs={{0,1},{1,0},{2,3},{3,2},{4,5},{5,4},{6,7},{7,6}} | collective-permute-start | bytes 9437192 | tf_op jit(solution)/shard_map/ppermute | solution.py:215
  1093.4 22.7 %collective-permute-start.21 = (bf16[2048,768]{1,0:T(8,128)(2,1)}, bf16[2048,768]{1,0:T(8,128)(2,1)S(1)}, u32[]{:S(2)}, u32[]{:S(2)}) collective-permute-start(bf16[2048,768]{1,0:T(8,128)(2,1)} %collective-permute-done.16), channel_id=1, source_target_pairs={{0,1},{1,0},{2,3},{3,2},{4,5},{5,4},{6,7},{7,6}} | collective-permute-start | bytes 9437192 | tf_op jit(solution)/shard_map/ppermute | solution.py:215
  1093.4 22.7 %collective-permute-start.22 = (bf16[2048,768]{1,0:T(8,128)(2,1)}, bf16[2048,768]{1,0:T(8,128)(2,1)S(1)}, u32[]{:S(2)}, u32[]{:S(2)}) collective-permute-start(bf16[2048,768]{1,0:T(8,128)(2,1)} %collective-permute-done.17), channel_id=1, source_target_pairs={{0,1},{1,0},{2,3},{3,2},{4,5},{5,4},{6,7},{7,6}} | collective-permute-start | bytes 9437192 | tf_op jit(solution)/shard_map/ppermute | solution.py:215
  1094.0 22.2 %collective-permute-start.23 = (bf16[2048,768]{1,0:T(8,128)(2,1)S(1)}, bf16[2048,768]{1,0:T(8,128)(2,1)S(1)}, u32[]{:S(2)}, u32[]{:S(2)}) collective-permute-start(bf16[2048,768]{1,0:T(8,128)(2,1)S(1)} %collective-permute-done.18), channel_id=1, source_target_pairs={{0,1},{1,0},{2,3},{3,2},{4,5},{5,4},{6,7},{7,6}} | collective-permute-start | bytes 9437192 | tf_op jit(solution)/shard_map/ppermute | solution.py:215
  1108.2 13.4 collective-permute-start.14
  1114.3 7.3 collective-permute-start.19
  1116.1 5.5 collective-permute-start.9
  1187.7 204.1 %collective-permute-start = (bf16[3072,768]{1,0:T(8,128)(2,1)}, bf16[3072,768]{1,0:T(8,128)(2,1)}, u32[]{:S(2)}, u32[]{:S(2)}) collective-permute-start(bf16[3072,768]{1,0:T(8,128)(2,1)} %branch_0_fun.5), channel_id=1, source_target_pairs={{0,1},{1,0},{2,3},{3,2},{4,5},{5,4},{6,7},{7,6}} | collective-permute-start | bytes 14155784 | tf_op jit(solution)/shard_map/cond/branch_0_fun/ppermute | solution.py:230
  1257.8 133.9 %collective-permute-start.1 = (bf16[3072,768]{1,0:T(8,128)(2,1)}, bf16[3072,768]{1,0:T(8,128)(2,1)}, u32[]{:S(2)}, u32[]{:S(2)}) collective-permute-start(bf16[3072,768]{1,0:T(8,128)(2,1)} %branch_0_fun.6), channel_id=1, source_target_pairs={{0,2},{1,3},{2,0},{3,1},{4,6},{5,7},{6,4},{7,5}} | collective-permute-start | bytes 14155784 | tf_op jit(solution)/shard_map/cond/branch_0_fun/ppermute | solution.py:230
  1322.2 140.3 %collective-permute-start.2 = (bf16[3072,768]{1,0:T(8,128)(2,1)}, bf16[3072,768]{1,0:T(8,128)(2,1)}, u32[]{:S(2)}, u32[]{:S(2)}) collective-permute-start(bf16[3072,768]{1,0:T(8,128)(2,1)} %branch_0_fun.7), channel_id=1, source_target_pairs={{0,3},{1,2},{2,1},{3,0},{4,7},{5,6},{6,5},{7,4}} | collective-permute-start | bytes 14155784 | tf_op jit(solution)/shard_map/cond/branch_0_fun/ppermute | solution.py:230
  1532.0 46.1 %copy-start.4 = (bf16[2048,768]{1,0:T(8,128)(2,1)S(1)}, bf16[2048,768]{1,0:T(8,128)(2,1)}, u32[]{:S(2)}) copy-start(bf16[2048,768]{1,0:T(8,128)(2,1)} %get-tuple-element.278) | copy-start | bytes 9437188 | tf_op jit(solution)/shard_map/conditional
  1532.0 46.1 %copy-start.67 = (f32[8192]{0:T(1024)S(1)}, f32[8192]{0:T(1024)}, u32[]{:S(2)}) copy-start(f32[8192]{0:T(1024)} %get-tuple-element.316) | copy-start | bytes 98308 | tf_op jit(solution)/shard_map/conditional
  1532.0 46.1 %copy-start.70 = (f32[8192]{0:T(1024)S(1)}, f32[8192]{0:T(1024)}, u32[]{:S(2)}) copy-start(f32[8192]{0:T(1024)} %get-tuple-element.280) | copy-start | bytes 98308 | tf_op jit(solution)/shard_map/conditional
  (114 other events, 1229.6 us)
Sparse Core Ops, SparseCore 0:
  17.3 60.7 all-gather.18
  79.6 60.3 all-gather.20
  141.5 60.1 all-gather.22
  203.0 60.1 all-gather.24
  264.6 221.9 all-gather.26
  488.0 221.9 all-gather.28
  1609.2 294.7 all-gather.16
